TPU v7x, 32 devices: a whole 2x2x4 slice. The times are simulated.
32 devices in a mesh: section: 2 (over x), fsdp: 16 (over z, y, core).
Axes of the slice: x: 2, y: 2, z: 4, core: 2. Of those that a mesh axis runs over, the one named last changes fastest.
Arguments:
- tokens: bfloat16 [6, 512, 4096], P(None, 'fsdp'), may hold values from -6 to 6
- cotangent: bfloat16 [6, 512, 4096], P(None, 'fsdp'), may hold values from -6 to 6
- order: int32 [6], replicated, may hold values from 0 to 5, each once
- w_value: bfloat16 [2, 4096, 512], P('section', 'fsdp'), may hold values from -0.09375 to 0.09375
- w_out: bfloat16 [2, 512, 4096], P('section', None, 'fsdp'), may hold values from -0.25 to 0.25
- adapter_down: bfloat16 [2, 4096, 128], P('section', 'fsdp'), may hold values from -0.09375 to 0.09375
- adapter_up: bfloat16 [2, 128, 512], P('section', None, 'fsdp'), may hold values from -0.5 to 0.5
Outputs:
- input_grads: bfloat16 [2, 6, 512, 4096], P('section', None, 'fsdp')
- grad_down: float32 [2, 4096, 128], P('section', 'fsdp')
- grad_up: float32 [2, 128, 512], P('section', None, 'fsdp')
Inputs may be any that keep to these rules, and one draw needn't show every extreme that they name: order names each microbatch 0 .. 5 exactly once.
All inputs are finite; a program needn't handle non-finite values.
Results may differ from a plain program's by a relative error of at most 0.02.
Values may be sent and summed in bfloat16 or wider, within the bound.
A program may use at most 128 MiB of HBM per device.

v0:
```python
import jax
import jax.numpy as jnp
from jax import lax
from jax.sharding import PartitionSpec as P

epsilon = 1e-05


def from_behind(block, axis, distance):
    devices = range(lax.axis_size(axis))
    route = [(i - distance, i) for i in devices if i - distance in devices]
    return lax.ppermute(block, axis, route)


def layer_forward(inputs, w_val, w_proj, a_down, a_up):
    widened = inputs.astype(jnp.float32)
    inverse = lax.rsqrt(jnp.mean(widened * widened, axis=-1, keepdims=True) + epsilon)
    normed = (widened * inverse).astype(jnp.bfloat16)
    low = jnp.dot(normed, a_down, preferred_element_type=jnp.float32).astype(jnp.bfloat16)
    values = (
        jnp.dot(normed, w_val, preferred_element_type=jnp.float32)
        + jnp.dot(low, a_up, preferred_element_type=jnp.float32)
    ).astype(jnp.bfloat16)
    outputs = (widened + jnp.dot(values, w_proj, preferred_element_type=jnp.float32)).astype(
        jnp.bfloat16
    )
    return (outputs, normed, low, inverse)


def layer_backward(inputs, inverse, upstream, w_val, w_proj, a_down, a_up):
    d_values = jnp.dot(upstream, w_proj.T, preferred_element_type=jnp.float32).astype(jnp.bfloat16)
    d_low = jnp.dot(d_values, a_up.T, preferred_element_type=jnp.float32).astype(jnp.bfloat16)
    d_normed = jnp.dot(d_values, w_val.T, preferred_element_type=jnp.float32) + jnp.dot(
        d_low, a_down.T, preferred_element_type=jnp.float32
    )
    widened = inputs.astype(jnp.float32)
    project = jnp.mean(d_normed * widened, axis=-1, keepdims=True)
    d_inputs = upstream.astype(jnp.float32) + inverse * (
        d_normed - widened * inverse * inverse * project
    )
    return (d_inputs.astype(jnp.bfloat16), d_values, d_low)


def store(buffer, item, clipped, in_range):
    previous = lax.dynamic_index_in_dim(buffer, clipped, 0, keepdims=False)
    return lax.dynamic_update_index_in_dim(buffer, jnp.where(in_range, item, previous), clipped, 0)


def contract_rows(left, right):
    return lax.dot_general(
        left, right, (((0,), (0,)), ((), ())), preferred_element_type=jnp.float32
    )


def body(tokens, cotangent, order, w_value, w_out, adapter_down, adapter_up):
    sections = lax.axis_size("section")
    position = lax.axis_index("section")
    count_micro = tokens.shape[0]
    local_tokens = tokens.shape[1]
    features = tokens.shape[2]
    rank = adapter_down.shape[2]
    gathered = (
        lax.all_gather(w_value, "fsdp", axis=1, tiled=True),
        lax.all_gather(w_out, "fsdp", axis=2, tiled=True),
        lax.all_gather(adapter_down, "fsdp", axis=1, tiled=True),
        lax.all_gather(adapter_up, "fsdp", axis=2, tiled=True),
    )
    full_val = gathered[0][0]
    full_proj = gathered[1][0]
    full_down = gathered[2][0]
    full_up = gathered[3][0]
    value_width = full_val.shape[1]
    moments = jnp.arange(count_micro + sections - 1, dtype=jnp.int32)

    def run_forward(inputs):
        return layer_forward(inputs, full_val, full_proj, full_down, full_up)

    def skip_forward(inputs):
        return (
            jnp.zeros((local_tokens, features), jnp.bfloat16),
            jnp.zeros((local_tokens, features), jnp.bfloat16),
            jnp.zeros((local_tokens, rank), jnp.bfloat16),
            jnp.zeros((local_tokens, 1), jnp.float32),
        )

    def forward_step(carry, moment):
        incoming, keep_in, keep_norm, keep_low, keep_inv = carry
        index_slot = moment - position
        in_range = (index_slot >= 0) & (index_slot < count_micro)
        clipped = jnp.clip(index_slot, 0, count_micro - 1)
        entering = tokens[order[clipped]]
        inputs = jnp.where(position == 0, entering, incoming)
        outputs, normed, low, inverse = lax.cond(in_range, run_forward, skip_forward, inputs)
        keep_in = store(keep_in, inputs, clipped, in_range)
        keep_norm = store(keep_norm, normed, clipped, in_range)
        keep_low = store(keep_low, low, clipped, in_range)
        keep_inv = store(keep_inv, inverse, clipped, in_range)
        passed = from_behind(outputs, "section", 1)
        return ((passed, keep_in, keep_norm, keep_low, keep_inv), None)

    start_fwd = (
        jnp.zeros((local_tokens, features), jnp.bfloat16),
        jnp.zeros(tokens.shape, jnp.bfloat16),
        jnp.zeros(tokens.shape, jnp.bfloat16),
        jnp.zeros((count_micro, local_tokens, rank), jnp.bfloat16),
        jnp.zeros((count_micro, local_tokens, 1), jnp.float32),
    )
    carried, unused = lax.scan(forward_step, start_fwd, moments)
    saved_in, saved_norm, saved_low, saved_inv = (carried[1], carried[2], carried[3], carried[4])

    def run_backward(operands):
        inputs, inverse, upstream = operands
        return layer_backward(inputs, inverse, upstream, full_val, full_proj, full_down, full_up)

    def skip_backward(operands):
        return (
            jnp.zeros((local_tokens, features), jnp.bfloat16),
            jnp.zeros((local_tokens, value_width), jnp.bfloat16),
            jnp.zeros((local_tokens, rank), jnp.bfloat16),
        )

    def backward_step(carry, moment):
        incoming, keep_dv, keep_dlow, keep_dx = carry
        index_slot = moment - (sections - 1 - position)
        in_range = (index_slot >= 0) & (index_slot < count_micro)
        clipped = jnp.clip(index_slot, 0, count_micro - 1)
        entering = cotangent[order[clipped]]
        upstream = jnp.where(position == sections - 1, entering, incoming)
        inputs = lax.dynamic_index_in_dim(saved_in, clipped, 0, keepdims=False)
        inverse = lax.dynamic_index_in_dim(saved_inv, clipped, 0, keepdims=False)
        d_inputs, d_values, d_low = lax.cond(
            in_range, run_backward, skip_backward, (inputs, inverse, upstream)
        )
        keep_dv = store(keep_dv, d_values, clipped, in_range)
        keep_dlow = store(keep_dlow, d_low, clipped, in_range)
        keep_dx = store(keep_dx, d_inputs, clipped, in_range)
        passed = from_behind(d_inputs, "section", -1)
        return ((passed, keep_dv, keep_dlow, keep_dx), None)

    start_bwd = (
        jnp.zeros((local_tokens, features), jnp.bfloat16),
        jnp.zeros((count_micro, local_tokens, value_width), jnp.bfloat16),
        jnp.zeros((count_micro, local_tokens, rank), jnp.bfloat16),
        jnp.zeros(tokens.shape, jnp.bfloat16),
    )
    carried_back, unused_back = lax.scan(backward_step, start_bwd, moments)
    saved_dv, saved_dlow, saved_dx = (carried_back[1], carried_back[2], carried_back[3])
    normed_flat = saved_norm.reshape(-1, features)
    low_flat = saved_low.reshape(-1, rank)
    dv_flat = saved_dv.reshape(-1, value_width)
    dlow_flat = saved_dlow.reshape(-1, rank)
    share_down = features // lax.axis_size("fsdp")
    share_up = value_width // lax.axis_size("fsdp")
    block_rows = share_down + share_up
    blocks = block_rows * lax.axis_size("fsdp") // block_rows
    part_down = contract_rows(normed_flat, dlow_flat).reshape(blocks, share_down, rank)
    part_up = contract_rows(dv_flat, low_flat).reshape(blocks, share_up, rank)
    combined = lax.psum_scatter(
        jnp.concatenate([part_down, part_up], axis=1).reshape(
            block_rows * lax.axis_size("fsdp"), rank
        ),
        "fsdp",
        scatter_dimension=0,
        tiled=True,
    )
    grad_down = combined[:share_down]
    grad_up_rows = combined[share_down:]
    return (saved_dx[None], grad_down[None], grad_up_rows.T[None])


def solution(mesh):
    return jax.shard_map(
        body,
        mesh=mesh,
        in_specs=(
            P(None, "fsdp", None),
            P(None, "fsdp", None),
            P(),
            P("section", "fsdp", None),
            P("section", None, "fsdp"),
            P("section", "fsdp", None),
            P("section", None, "fsdp"),
        ),
        out_specs=(
            P("section", None, "fsdp", None),
            P("section", "fsdp", None),
            P("section", None, "fsdp"),
        ),
        check_vma=False,
    )
```

profile of v0, /device:TPU:0, one launch (start us, length us, event | category | flops | bytes accessed | tf_op | source)
XLA Modules:
  0.0 519.8 jit_solution(2952609717365641227)
XLA Ops:
  9.4 23.7 %all_gather.14 = bf16[1,128,512]{1,2,0:T(8,128)(2,1)S(1)} all-gather(bf16[1,128,32]{1,2,0:T(8,128)(2,1)} %param.21), channel_id=1, replica_groups=mesh['section'=2,'fsdp'=16] {'fsdp'}, dimensions={2}, use_global_device_ids=true | all-gather | bytes 139264 | tf_op jit(solution)/shard_map/all_gather | solution.py:66
  33.3 17.4 %all-gather.6.cloned.1.call-done = bf16[1,4096,128]{2,1,0:T(8,128)(2,1)} async-done(((bf16[1,256,128]{2,1,0:T(8,128)(2,1)}), bf16[1,4096,128]{2,1,0:T(8,128)(2,1)}) %all-gather.6.cloned.1.call-update) | async-done | bytes 1048592 | tf_op jit(solution)/shard_map/all_gather | solution.py:65
  50.7 51.5 %all-gather.4.cloned.1.call-done = bf16[1,4096,512]{2,1,0:T(8,128)(2,1)} async-done(((bf16[1,256,512]{2,1,0:T(8,128)(2,1)}), bf16[1,4096,512]{2,1,0:T(8,128)(2,1)}) %all-gather.4.cloned.1.call-update) | async-done | bytes 4194320 | tf_op jit(solution)/shard_map/all_gather | solution.py:63
  102.3 53.2 %all-gather.8.cloned.1.call-done = bf16[1,512,4096]{2,1,0:T(8,128)(2,1)} async-done(((bf16[1,512,256]{2,1,0:T(8,128)(2,1)}), bf16[1,512,4096]{2,1,0:T(8,128)(2,1)}) %all-gather.8.cloned.1.call-update) | async-done | bytes 4194320 | tf_op jit(solution)/shard_map/all_gather | solution.py:64
  157.7 152.0 %while.37 = (s32[]{:T(128)}, bf16[32,4096]{1,0:T(8,128)(2,1)S(1)}, bf16[6,32,4096]{2,1,0:T(8,128)(2,1)S(1)}, bf16[6,32,4096]{2,1,0:T(8,128)(2,1)}, bf16[6,32,128...) while((s32[]{:T(128)}, bf16[32,4096]{1,0:T(8,128)(2,1)S(1)}, ...), condition=%wide.region_4.5_spmd, body=%wide.region_0.4_spmd.sunk | while | flops 307798080 | bytes 17886068 | solution.py:108
  162.6 8.1 %conditional.4 = (bf16[32,4096]{1,0:T(8,128)(2,1)}, bf16[32,4096]{1,0:T(8,128)(2,1)S(1)}, bf16[32,128]{1,0:T(8,128)(2,1)}, f32[32,1]{0,1:T(1,128)S(1)}) conditional(s32[]{:T(128)} %convert_element_type.72, () %tuple.79, (bf16[32,4096]{1,0:T(8,128)(2,1)S(1)}, bf16[4096,512]{1,0:T(8,128)(2,1)}, bf16[4096,128]{1,0:T(8,128)(2,1)S(1)}, ...), branch_computations={%region_1.1_spmd, %region_2.3_spmd} | conditional | flops 307400736 | bytes 13648600 | solution.py:93
  183.5 8.1 %conditional.4 = (bf16[32,4096]{1,0:T(8,128)(2,1)}, bf16[32,4096]{1,0:T(8,128)(2,1)S(1)}, bf16[32,128]{1,0:T(8,128)(2,1)}, f32[32,1]{0,1:T(1,128)S(1)}) conditional(s32[]{:T(128)} %convert_element_type.72, () %tuple.79, (bf16[32,4096]{1,0:T(8,128)(2,1)S(1)}, bf16[4096,512]{1,0:T(8,128)(2,1)}, bf16[4096,128]{1,0:T(8,128)(2,1)S(1)}, ...), branch_computations={%region_1.1_spmd, %region_2.3_spmd} | conditional | flops 307400736 | bytes 13648600 | solution.py:93
  191.6 4.3 collective-permute-start
  206.5 8.1 %conditional.4 = (bf16[32,4096]{1,0:T(8,128)(2,1)}, bf16[32,4096]{1,0:T(8,128)(2,1)S(1)}, bf16[32,128]{1,0:T(8,128)(2,1)}, f32[32,1]{0,1:T(1,128)S(1)}) conditional(s32[]{:T(128)} %convert_element_type.72, () %tuple.79, (bf16[32,4096]{1,0:T(8,128)(2,1)S(1)}, bf16[4096,512]{1,0:T(8,128)(2,1)}, bf16[4096,128]{1,0:T(8,128)(2,1)S(1)}, ...), branch_computations={%region_1.1_spmd, %region_2.3_spmd} | conditional | flops 307400736 | bytes 13648600 | solution.py:93
  214.6 4.3 collective-permute-start
  228.6 8.1 %conditional.4 = (bf16[32,4096]{1,0:T(8,128)(2,1)}, bf16[32,4096]{1,0:T(8,128)(2,1)S(1)}, bf16[32,128]{1,0:T(8,128)(2,1)}, f32[32,1]{0,1:T(1,128)S(1)}) conditional(s32[]{:T(128)} %convert_element_type.72, () %tuple.79, (bf16[32,4096]{1,0:T(8,128)(2,1)S(1)}, bf16[4096,512]{1,0:T(8,128)(2,1)}, bf16[4096,128]{1,0:T(8,128)(2,1)S(1)}, ...), branch_computations={%region_1.1_spmd, %region_2.3_spmd} | conditional | flops 307400736 | bytes 13648600 | solution.py:93
  250.1 8.1 %conditional.4 = (bf16[32,4096]{1,0:T(8,128)(2,1)}, bf16[32,4096]{1,0:T(8,128)(2,1)S(1)}, bf16[32,128]{1,0:T(8,128)(2,1)}, f32[32,1]{0,1:T(1,128)S(1)}) conditional(s32[]{:T(128)} %convert_element_type.72, () %tuple.79, (bf16[32,4096]{1,0:T(8,128)(2,1)S(1)}, bf16[4096,512]{1,0:T(8,128)(2,1)}, bf16[4096,128]{1,0:T(8,128)(2,1)S(1)}, ...), branch_computations={%region_1.1_spmd, %region_2.3_spmd} | conditional | flops 307400736 | bytes 13648600 | solution.py:93
  258.2 4.3 collective-permute-start
  271.6 8.1 %conditional.4 = (bf16[32,4096]{1,0:T(8,128)(2,1)}, bf16[32,4096]{1,0:T(8,128)(2,1)S(1)}, bf16[32,128]{1,0:T(8,128)(2,1)}, f32[32,1]{0,1:T(1,128)S(1)}) conditional(s32[]{:T(128)} %convert_element_type.72, () %tuple.79, (bf16[32,4096]{1,0:T(8,128)(2,1)S(1)}, bf16[4096,512]{1,0:T(8,128)(2,1)}, bf16[4096,128]{1,0:T(8,128)(2,1)S(1)}, ...), branch_computations={%region_1.1_spmd, %region_2.3_spmd} | conditional | flops 307400736 | bytes 13648600 | solution.py:93
  294.4 11.1 %collective-permute-start = (bf16[32,4096]{1,0:T(8,128)(2,1)}, bf16[32,4096]{1,0:T(8,128)(2,1)S(1)}, u32[]{:S(2)}, u32[]{:S(2)}) collective-permute-start(bf16[32,4096]{1,0:T(8,128)(2,1)} %get-tuple-element.743), channel_id=1, source_target_pairs={{0,16},{1,17},{2,18},{3,19},{4,20},{5,21},{6,22},{7,23},{8,24},{9,... | collective-permute-start | bytes 786440 | tf_op jit(solution)/shard_map/while/body/eval_jaxpr/ppermute | solution.py:12
  311.6 133.9 %while.38 = (s32[]{:T(128)}, bf16[32,4096]{1,0:T(8,128)(2,1)S(1)}, bf16[6,32,512]{2,1,0:T(8,128)(2,1)S(1)}, bf16[6,32,128]{2,1,0:T(8,128)(2,1)}, bf16[6,32,4096]...) while((s32[]{:T(128)}, bf16[32,4096]{1,0:T(8,128)(2,1)S(1)}, ...), condition=%wide.region_9.10_spmd, body=%wide.region_5.9_spmd.sunk | while | flops 308322304 | bytes 33287160 | solution.py:146
  317.3 13.2 %collective-permute-done.1 = bf16[32,4096]{1,0:T(8,128)(2,1)S(1)} collective-permute-done((bf16[32,4096]{1,0:T(8,128)(2,1)S(1)}, bf16[32,4096]{1,0:T(8,128)(2,1)S(1)}, u32[]{:S(2)}, u32[]{:S(2)}) %collective-permute-start.1) | collective-permute-done | bytes 262176 | tf_op jit(solution)/shard_map/while/body/eval_jaxpr/ppermute | solution.py:12
  331.8 9.6 %conditional.5 = (bf16[32,4096]{1,0:T(8,128)(2,1)S(1)}, bf16[32,512]{1,0:T(8,128)(2,1)S(1)}, bf16[32,128]{1,0:T(8,128)(2,1)S(1)}) conditional(s32[]{:T(128)} %convert_element_type.73, () %tuple.82, (pred[]{:T(512)}, s32[6]{0:T(128)S(1)}, s32[]{:T(128)}, bf16[6,32,4096]{2,1,0:T(8,128)(2,1)}, bf16[32,4096]{1,0:T(8,128)(2,1)S(1)}, ...), branch_computations={%region_6.6_spmd, %region_7.8_spmd} | conditional | flops 308170752 | bytes 30721640 | solution.py:131
  351.0 9.6 %conditional.5 = (bf16[32,4096]{1,0:T(8,128)(2,1)S(1)}, bf16[32,512]{1,0:T(8,128)(2,1)S(1)}, bf16[32,128]{1,0:T(8,128)(2,1)S(1)}) conditional(s32[]{:T(128)} %convert_element_type.73, () %tuple.82, (pred[]{:T(512)}, s32[6]{0:T(128)S(1)}, s32[]{:T(128)}, bf16[6,32,4096]{2,1,0:T(8,128)(2,1)}, bf16[32,4096]{1,0:T(8,128)(2,1)S(1)}, ...), branch_computations={%region_6.6_spmd, %region_7.8_spmd} | conditional | flops 308170752 | bytes 30721640 | solution.py:131
  370.1 9.6 %conditional.5 = (bf16[32,4096]{1,0:T(8,128)(2,1)S(1)}, bf16[32,512]{1,0:T(8,128)(2,1)S(1)}, bf16[32,128]{1,0:T(8,128)(2,1)S(1)}) conditional(s32[]{:T(128)} %convert_element_type.73, () %tuple.82, (pred[]{:T(512)}, s32[6]{0:T(128)S(1)}, s32[]{:T(128)}, bf16[6,32,4096]{2,1,0:T(8,128)(2,1)}, bf16[32,4096]{1,0:T(8,128)(2,1)S(1)}, ...), branch_computations={%region_6.6_spmd, %region_7.8_spmd} | conditional | flops 308170752 | bytes 30721640 | solution.py:131
  389.3 9.6 %conditional.5 = (bf16[32,4096]{1,0:T(8,128)(2,1)S(1)}, bf16[32,512]{1,0:T(8,128)(2,1)S(1)}, bf16[32,128]{1,0:T(8,128)(2,1)S(1)}) conditional(s32[]{:T(128)} %convert_element_type.73, () %tuple.82, (pred[]{:T(512)}, s32[6]{0:T(128)S(1)}, s32[]{:T(128)}, bf16[6,32,4096]{2,1,0:T(8,128)(2,1)}, bf16[32,4096]{1,0:T(8,128)(2,1)S(1)}, ...), branch_computations={%region_6.6_spmd, %region_7.8_spmd} | conditional | flops 308170752 | bytes 30721640 | solution.py:131
  408.5 9.6 %conditional.5 = (bf16[32,4096]{1,0:T(8,128)(2,1)S(1)}, bf16[32,512]{1,0:T(8,128)(2,1)S(1)}, bf16[32,128]{1,0:T(8,128)(2,1)S(1)}) conditional(s32[]{:T(128)} %convert_element_type.73, () %tuple.82, (pred[]{:T(512)}, s32[6]{0:T(128)S(1)}, s32[]{:T(128)}, bf16[6,32,4096]{2,1,0:T(8,128)(2,1)}, bf16[32,4096]{1,0:T(8,128)(2,1)S(1)}, ...), branch_computations={%region_6.6_spmd, %region_7.8_spmd} | conditional | flops 308170752 | bytes 30721640 | solution.py:131
  427.6 9.6 %conditional.5 = (bf16[32,4096]{1,0:T(8,128)(2,1)S(1)}, bf16[32,512]{1,0:T(8,128)(2,1)S(1)}, bf16[32,128]{1,0:T(8,128)(2,1)S(1)}) conditional(s32[]{:T(128)} %convert_element_type.73, () %tuple.82, (pred[]{:T(512)}, s32[6]{0:T(128)S(1)}, s32[]{:T(128)}, bf16[6,32,4096]{2,1,0:T(8,128)(2,1)}, bf16[32,4096]{1,0:T(8,128)(2,1)S(1)}, ...), branch_computations={%region_6.6_spmd, %region_7.8_spmd} | conditional | flops 308170752 | bytes 30721640 | solution.py:131
  449.8 60.6 %reduce-scatter.2.cloned.1.call-done = f32[288,128]{1,0:T(8,128)} async-done(((f32[4608,128]{1,0:T(8,128)}), f32[288,128]{1,0:T(8,128)}) %reduce-scatter.2.cloned.1.call-update) | async-done | bytes 147472 | tf_op jit(solution)/shard_map/reduce_scatter | solution.py:158
  (351 shorter events, 227.8 us)
Async XLA Ops:
  7.2 43.6 %all-gather.6.cloned.1.call-start = ((), (), s32[]{:S(2)}) async-start(), calls=%async_computation.2 | async-start | bytes 1114112 | tf_op jit(solution)/shard_map/all_gather | solution.py:65
  7.9 94.4 %all-gather.4.cloned.1.call-start = ((), (), s32[]{:S(2)}) async-start(), calls=%async_computation.1 | async-start | bytes 4456448 | tf_op jit(solution)/shard_map/all_gather | solution.py:63
  8.6 146.8 %all-gather.8.cloned.1.call-start = ((), (), s32[]{:S(2)}) async-start(), calls=%async_computation.3 | async-start | bytes 4456448 | tf_op jit(solution)/shard_map/all_gather | solution.py:64
  9.4 501.0 %reduce-scatter.2.cloned.1.call-start = ((), (), s32[]{:S(2)}) async-start(), calls=%async_computation.4 | async-start | bytes 2506752 | tf_op jit(solution)/shard_map/reduce_scatter | solution.py:158
  170.7 7.8 %collective-permute-start = (bf16[32,4096]{1,0:T(8,128)(2,1)}, bf16[32,4096]{1,0:T(8,128)(2,1)S(1)}, u32[]{:S(2)}, u32[]{:S(2)}) collective-permute-start(bf16[32,4096]{1,0:T(8,128)(2,1)} %get-tuple-element.743), channel_id=1, source_target_pairs={{0,16},{1,17},{2,18},{3,19},{4,20},{5,21},{6,22},{7,23},{8,24},{9,... | collective-permute-start | bytes 786440 | tf_op jit(solution)/shard_map/while/body/eval_jaxpr/ppermute | solution.py:12
  191.6 10.0 %collective-permute-start = (bf16[32,4096]{1,0:T(8,128)(2,1)}, bf16[32,4096]{1,0:T(8,128)(2,1)S(1)}, u32[]{:S(2)}, u32[]{:S(2)}) collective-permute-start(bf16[32,4096]{1,0:T(8,128)(2,1)} %get-tuple-element.743), channel_id=1, source_target_pairs={{0,16},{1,17},{2,18},{3,19},{4,20},{5,21},{6,22},{7,23},{8,24},{9,... | collective-permute-start | bytes 786440 | tf_op jit(solution)/shard_map/while/body/eval_jaxpr/ppermute | solution.py:12
  214.6 9.1 %collective-permute-start = (bf16[32,4096]{1,0:T(8,128)(2,1)}, bf16[32,4096]{1,0:T(8,128)(2,1)S(1)}, u32[]{:S(2)}, u32[]{:S(2)}) collective-permute-start(bf16[32,4096]{1,0:T(8,128)(2,1)} %get-tuple-element.743), channel_id=1, source_target_pairs={{0,16},{1,17},{2,18},{3,19},{4,20},{5,21},{6,22},{7,23},{8,24},{9,... | collective-permute-start | bytes 786440 | tf_op jit(solution)/shard_map/while/body/eval_jaxpr/ppermute | solution.py:12
  236.7 8.5 %collective-permute-start = (bf16[32,4096]{1,0:T(8,128)(2,1)}, bf16[32,4096]{1,0:T(8,128)(2,1)S(1)}, u32[]{:S(2)}, u32[]{:S(2)}) collective-permute-start(bf16[32,4096]{1,0:T(8,128)(2,1)} %get-tuple-element.743), channel_id=1, source_target_pairs={{0,16},{1,17},{2,18},{3,19},{4,20},{5,21},{6,22},{7,23},{8,24},{9,... | collective-permute-start | bytes 786440 | tf_op jit(solution)/shard_map/while/body/eval_jaxpr/ppermute | solution.py:12
  258.2 8.5 %collective-permute-start = (bf16[32,4096]{1,0:T(8,128)(2,1)}, bf16[32,4096]{1,0:T(8,128)(2,1)S(1)}, u32[]{:S(2)}, u32[]{:S(2)}) collective-permute-start(bf16[32,4096]{1,0:T(8,128)(2,1)} %get-tuple-element.743), channel_id=1, source_target_pairs={{0,16},{1,17},{2,18},{3,19},{4,20},{5,21},{6,22},{7,23},{8,24},{9,... | collective-permute-start | bytes 786440 | tf_op jit(solution)/shard_map/while/body/eval_jaxpr/ppermute | solution.py:12
  279.7 8.5 %collective-permute-start = (bf16[32,4096]{1,0:T(8,128)(2,1)}, bf16[32,4096]{1,0:T(8,128)(2,1)S(1)}, u32[]{:S(2)}, u32[]{:S(2)}) collective-permute-start(bf16[32,4096]{1,0:T(8,128)(2,1)} %get-tuple-element.743), channel_id=1, source_target_pairs={{0,16},{1,17},{2,18},{3,19},{4,20},{5,21},{6,22},{7,23},{8,24},{9,... | collective-permute-start | bytes 786440 | tf_op jit(solution)/shard_map/while/body/eval_jaxpr/ppermute | solution.py:12
  294.4 15.2 %collective-permute-start = (bf16[32,4096]{1,0:T(8,128)(2,1)}, bf16[32,4096]{1,0:T(8,128)(2,1)S(1)}, u32[]{:S(2)}, u32[]{:S(2)}) collective-permute-start(bf16[32,4096]{1,0:T(8,128)(2,1)} %get-tuple-element.743), channel_id=1, source_target_pairs={{0,16},{1,17},{2,18},{3,19},{4,20},{5,21},{6,22},{7,23},{8,24},{9,... | collective-permute-start | bytes 786440 | tf_op jit(solution)/shard_map/while/body/eval_jaxpr/ppermute | solution.py:12
  313.0 17.6 %collective-permute-start.1 = (bf16[32,4096]{1,0:T(8,128)(2,1)S(1)}, bf16[32,4096]{1,0:T(8,128)(2,1)S(1)}, u32[]{:S(2)}, u32[]{:S(2)}) collective-permute-start(bf16[32,4096]{1,0:T(8,128)(2,1)S(1)} %get-tuple-element.764), channel_id=1, source_target_pairs={{16,0},{17,1},{18,2},{19,3},{20,4},{21,5},{22,6},{23,7},{24,8},{25... | collective-permute-start | bytes 786440 | tf_op jit(solution)/shard_map/while/body/eval_jaxpr/ppermute | solution.py:12
  334.3 3.9 copy-start
  341.4 8.3 %collective-permute-start.1 = (bf16[32,4096]{1,0:T(8,128)(2,1)S(1)}, bf16[32,4096]{1,0:T(8,128)(2,1)S(1)}, u32[]{:S(2)}, u32[]{:S(2)}) collective-permute-start(bf16[32,4096]{1,0:T(8,128)(2,1)S(1)} %get-tuple-element.764), channel_id=1, source_target_pairs={{16,0},{17,1},{18,2},{19,3},{20,4},{21,5},{22,6},{23,7},{24,8},{25... | collective-permute-start | bytes 786440 | tf_op jit(solution)/shard_map/while/body/eval_jaxpr/ppermute | solution.py:12
  353.5 3.9 copy-start
  360.6 8.3 %collective-permute-start.1 = (bf16[32,4096]{1,0:T(8,128)(2,1)S(1)}, bf16[32,4096]{1,0:T(8,128)(2,1)S(1)}, u32[]{:S(2)}, u32[]{:S(2)}) collective-permute-start(bf16[32,4096]{1,0:T(8,128)(2,1)S(1)} %get-tuple-element.764), channel_id=1, source_target_pairs={{16,0},{17,1},{18,2},{19,3},{20,4},{21,5},{22,6},{23,7},{24,8},{25... | collective-permute-start | bytes 786440 | tf_op jit(solution)/shard_map/while/body/eval_jaxpr/ppermute | solution.py:12
  372.7 3.9 copy-start
  379.8 8.3 %collective-permute-start.1 = (bf16[32,4096]{1,0:T(8,128)(2,1)S(1)}, bf16[32,4096]{1,0:T(8,128)(2,1)S(1)}, u32[]{:S(2)}, u32[]{:S(2)}) collective-permute-start(bf16[32,4096]{1,0:T(8,128)(2,1)S(1)} %get-tuple-element.764), channel_id=1, source_target_pairs={{16,0},{17,1},{18,2},{19,3},{20,4},{21,5},{22,6},{23,7},{24,8},{25... | collective-permute-start | bytes 786440 | tf_op jit(solution)/shard_map/while/body/eval_jaxpr/ppermute | solution.py:12
  391.8 3.9 copy-start
  398.9 8.3 %collective-permute-start.1 = (bf16[32,4096]{1,0:T(8,128)(2,1)S(1)}, bf16[32,4096]{1,0:T(8,128)(2,1)S(1)}, u32[]{:S(2)}, u32[]{:S(2)}) collective-permute-start(bf16[32,4096]{1,0:T(8,128)(2,1)S(1)} %get-tuple-element.764), channel_id=1, source_target_pairs={{16,0},{17,1},{18,2},{19,3},{20,4},{21,5},{22,6},{23,7},{24,8},{25... | collective-permute-start | bytes 786440 | tf_op jit(solution)/shard_map/while/body/eval_jaxpr/ppermute | solution.py:12
  411.0 3.9 copy-start
  418.1 8.3 %collective-permute-start.1 = (bf16[32,4096]{1,0:T(8,128)(2,1)S(1)}, bf16[32,4096]{1,0:T(8,128)(2,1)S(1)}, u32[]{:S(2)}, u32[]{:S(2)}) collective-permute-start(bf16[32,4096]{1,0:T(8,128)(2,1)S(1)} %get-tuple-element.764), channel_id=1, source_target_pairs={{16,0},{17,1},{18,2},{19,3},{20,4},{21,5},{22,6},{23,7},{24,8},{25... | collective-permute-start | bytes 786440 | tf_op jit(solution)/shard_map/while/body/eval_jaxpr/ppermute | solution.py:12
  430.2 3.9 copy-start
  437.3 8.3 %collective-permute-start.1 = (bf16[32,4096]{1,0:T(8,128)(2,1)S(1)}, bf16[32,4096]{1,0:T(8,128)(2,1)S(1)}, u32[]{:S(2)}, u32[]{:S(2)}) collective-permute-start(bf16[32,4096]{1,0:T(8,128)(2,1)S(1)} %get-tuple-element.764), channel_id=1, source_target_pairs={{16,0},{17,1},{18,2},{19,3},{20,4},{21,5},{22,6},{23,7},{24,8},{25... | collective-permute-start | bytes 786440 | tf_op jit(solution)/shard_map/while/body/eval_jaxpr/ppermute | solution.py:12
  (39 other events, 88.7 us)
Sparse Core Ops, SparseCore 0:
  10.1 40.5 all-gather.5
  52.9 49.3 all-gather.3
  104.4 50.9 all-gather.7
  449.9 60.4 reduce-scatter.1
where the time goes:
time: 523 us; the launch traced here: 520 us
  waiting for transfers between devices  229 us (44%)
  matrix products  83.6 us (16%)
  local copies, waits for them, and re-layouts  48.7 us (9%)
  starting transfers between devices  43 us (8%)
  other arithmetic  41.6 us (8%)
  loops' own time  36 us (7%)
  blocking collectives  23.7 us (5%)
  between operations  13.8 us (3%)
    reduce_scatter x1, waiting for transfers between devices, body(): lax.psum_scatter(jnp.concatenate([part_down, part_up], axis=1).reshape(bl...  60.6 us
    all_gather x1, waiting for transfers between devices, body(): lax.all_gather(w_out, 'fsdp', axis=2, tiled=True)  53.2 us
    all_gather x1, waiting for transfers between devices, body(): lax.all_gather(w_value, 'fsdp', axis=1, tiled=True)  51.5 us
    ppermute x14, waiting for transfers between devices, from_behind(): return lax.ppermute(block, axis, route)  44.6 us
    ppermute x14, starting transfers between devices, from_behind(): return lax.ppermute(block, axis, route)  42.8 us
    dynamic_update_slice x49, other arithmetic, store(): lax.dynamic_update_index_in_dim(buffer, jnp.where(in_range, item, previou...  31.1 us
    all_gather x1, blocking collectives, body(): lax.all_gather(adapter_up, 'fsdp', axis=2, tiled=True)  23.7 us
    dynamic_slice x42, local copies, waits for them, and re-layouts, store(): previous = lax.dynamic_index_in_dim(buffer, clipped, 0, keepdims=False)  23.6 us
  transfers between devices with their start and end apart: 18, of which 18 were waited for; matrix products, arithmetic and copies ran while one was open for 9% of the time, Pallas kernels for 0%

commit v1 on v0

v1 whole, which is shorter than its diff:
```python
import jax
import jax.numpy as jnp
from jax import lax
from jax.sharding import PartitionSpec as P

epsilon = 1e-05


def widen_dot(left, right, dims=((1,), (0,))):
    return lax.dot_general(left, right, (dims, ((), ())), preferred_element_type=jnp.float32)


def gather_weights(w_value, w_out, adapter_down, adapter_up):
    sections = lax.axis_size("section")
    joined = jnp.concatenate([w_value[0], adapter_down[0]], axis=1)
    proj = w_out[0].T
    up = adapter_up[0].T

    def whole(block):
        full = lax.all_gather(block, ("section", "fsdp"), axis=0, tiled=True)
        return full.reshape(sections, -1, block.shape[1])

    return whole(joined), whole(proj), whole(up)


def body(tokens, cotangent, order, w_value, w_out, adapter_down, adapter_up):
    sections = lax.axis_size("section")
    position = lax.axis_index("section")
    micro, local, features = tokens.shape
    width = w_value.shape[2]
    joined, proj, up = gather_weights(w_value, w_out, adapter_down, adapter_up)

    current = tokens.reshape(micro * local, features)
    saved = []
    for layer in range(sections):
        widened = current.astype(jnp.float32)
        inverse = lax.rsqrt(jnp.mean(widened * widened, axis=-1, keepdims=True) + epsilon)
        normed = (widened * inverse).astype(jnp.bfloat16)
        last = layer == sections - 1
        if last:
            low = widen_dot(normed, joined[layer][:, width:]).astype(jnp.bfloat16)
        else:
            both = widen_dot(normed, joined[layer])
            low = both[:, width:].astype(jnp.bfloat16)
            values = (both[:, :width] + widen_dot(low, up[layer], ((1,), (1,)))).astype(jnp.bfloat16)
        saved.append((current, normed, low, inverse))
        if not last:
            current = (widened + widen_dot(values, proj[layer], ((1,), (1,)))).astype(jnp.bfloat16)

    upstream = cotangent.reshape(micro * local, features)
    grads, d_vals, d_lows = [], [], []
    for layer in reversed(range(sections)):
        inputs, normed, low, inverse = saved[layer]
        d_values = widen_dot(upstream, proj[layer]).astype(jnp.bfloat16)
        d_low = widen_dot(d_values, up[layer]).astype(jnp.bfloat16)
        d_normed = widen_dot(
            jnp.concatenate([d_values, d_low], axis=1), joined[layer], ((1,), (1,))
        )
        widened = inputs.astype(jnp.float32)
        project = jnp.mean(d_normed * widened, axis=-1, keepdims=True)
        upstream = (
            upstream.astype(jnp.float32)
            + inverse * (d_normed - widened * inverse * inverse * project)
        ).astype(jnp.bfloat16)
        grads.insert(0, upstream)
        d_vals.insert(0, d_values)
        d_lows.insert(0, d_low)

    def mine(items):
        chosen = items[0]
        for layer in range(1, sections):
            chosen = jnp.where(position == layer, items[layer], chosen)
        return chosen

    shares = lax.axis_size("fsdp")
    normed = mine([item[1] for item in saved])
    low = mine([item[2] for item in saved])
    part_down = widen_dot(normed, mine(d_lows), ((0,), (0,)))
    part_up = widen_dot(mine(d_vals), low, ((0,), (0,)))
    rank = low.shape[1]
    parts = jnp.concatenate(
        [part_down.reshape(shares, -1, rank), part_up.reshape(shares, -1, rank)], axis=1
    )
    combined = lax.psum_scatter(parts, "fsdp", scatter_dimension=0, tiled=True)[0]
    share_down = features // shares
    out = mine(grads).reshape(micro, local, features)[order]
    return (out[None], combined[:share_down][None], combined[share_down:].T[None])


def solution(mesh):
    return jax.shard_map(
        body,
        mesh=mesh,
        in_specs=(
            P(None, "fsdp", None),
            P(None, "fsdp", None),
            P(),
            P("section", "fsdp", None),
            P("section", None, "fsdp"),
            P("section", "fsdp", None),
            P("section", None, "fsdp"),
        ),
        out_specs=(
            P("section", None, "fsdp", None),
            P("section", "fsdp", None),
            P("section", None, "fsdp"),
        ),
        check_vma=False,
    )
```

time: 523 us -> 296 us (0.57)
  matrix products: 83.6 us -> 34.6 us
  waiting for transfers between devices: 229 us -> 183 us
  local copies, waits for them, and re-layouts: 48.7 us -> 5.48 us
  starting transfers between devices: 43 us -> 0.12 us
  loops' own time: 36 us -> 0 us
  other arithmetic: 41.6 us -> 12 us
  blocking collectives: 23.7 us -> 47.2 us
    dot_general x44 -> x10, matrix products: 83.6 us -> 34.6 us  [widen_dot(): lax.dot_general(left, right, (dims, ((), ())), preferred_element_type=jnp...]
    ppermute x14 -> x0, waiting for transfers between devices: 44.6 us -> none  [from_behind(): return lax.ppermute(block, axis, route)]
    ppermute x14 -> x0, starting transfers between devices: 42.8 us -> none  [from_behind(): return lax.ppermute(block, axis, route)]
    dynamic_slice x69 -> x0, local copies, waits for them, and re-layouts: 39.4 us -> none  [the longest x42 23.6 us: store(): previous = lax.dynamic_index_in_dim(buffer, clipped, 0, keepdims=False)]
    another operation x16 -> x0, loops' own time: 36 us -> none  [the longest x1 18.6 us: body(): carried, unused = lax.scan(forward_step, start_fwd, moments)]
    dynamic_update_slice x49 -> x0, other arithmetic: 31.1 us -> none  [store(): lax.dynamic_update_index_in_dim(buffer, jnp.where(in_range, item, previou...]
    all_gather x1, blocking collectives: 23.7 us -> 47.2 us  [whole(): full = lax.all_gather(block, ('section', 'fsdp'), axis=0, tiled=True)]
    reduce_scatter x1, waiting for transfers between devices: 60.6 us -> 54.1 us  [body(): lax.psum_scatter(parts, 'fsdp', scatter_dimension=0, tiled=True)[0]]
  transfers between devices with their start and end apart: 18 -> 3, of which waited for: 18 -> 3; matrix products, arithmetic and copies ran while one was open for 9% -> 5% of each run, Pallas kernels for 0% -> 0%
where the time goes in v1:
time: 296 us
  waiting for transfers between devices  183 us (62%)
  blocking collectives  47.2 us (16%)
  matrix products  34.6 us (12%)
  between operations  14 us (5%)
  other arithmetic  12 us (4%)
  local copies, waits for them, and re-layouts  5.48 us (2%)
    all_gather x2, waiting for transfers between devices, whole(): full = lax.all_gather(block, ('section', 'fsdp'), axis=0, tiled=True)  128 us
    reduce_scatter x1, waiting for transfers between devices, body(): lax.psum_scatter(parts, 'fsdp', scatter_dimension=0, tiled=True)[0]  54.1 us
    all_gather x1, blocking collectives, whole(): full = lax.all_gather(block, ('section', 'fsdp'), axis=0, tiled=True)  47.2 us
    dot_general x10, matrix products, widen_dot(): lax.dot_general(left, right, (dims, ((), ())), preferred_element_type=jnp...  34.6 us
  transfers between devices with their start and end apart: 3, of which 3 were waited for; matrix products, arithmetic and copies ran while one was open for 5% of the time, Pallas kernels for 0%

profile of v1, /device:TPU:0, one launch (start us, length us, event | category | flops | bytes accessed | tf_op | source)
XLA Modules:
  0.0 296.1 jit_solution(10536940691265955632)
XLA Ops:
  7.2 0.7 all-gather.5.cloned.1.call-update
  8.0 1.7 pad_maximum_fusion.1
  9.8 1.8 multiply_reduce_fusion.3
  11.7 47.2 %all_gather.10 = bf16[1024,128]{1,0:T(8,128)(2,1)} all-gather(bf16[32,128]{1,0:T(8,128)(2,1)} %bitcast.39), channel_id=1, replica_groups=mesh['section'=2,'fsdp'=16] {'section','fsdp'}, dimensions={0}, use_global_device_ids=true | all-gather | bytes 270336 | tf_op jit(solution)/shard_map/all_gather | solution.py:20
  58.9 0.4 multiply_convert_fusion.1
  59.3 44.6 %all-gather.5.cloned.1.call-done = bf16[8192,512]{0,1:T(8,128)(2,1)} async-done(((bf16[256,512]{0,1:T(8,128)(2,1)}), bf16[8192,512]{0,1:T(8,128)(2,1)}) %all-gather.5.cloned.1.call-update) | async-done | bytes 8388624 | tf_op jit(solution)/shard_map/all_gather | solution.py:20
  103.9 4.2 %fusion.21 = bf16[192,512]{1,0:T(8,128)(2,1)S(1)} fusion(bf16[192,4096]{1,0:T(8,128)(2,1)} %bitcast.33, bf16[8192,512]{0,1:T(8,128)(2,1)} %all-gather.5.cloned.1.call-done), kind=kOutput, calls=%fused_computation.31 | convolution fusion | flops 805404672 | bytes 5963776 | tf_op jit(solution)/shard_map/dot_general | solution.py:10
  108.4 83.3 %all-gather.3.cloned.1.call-done = bf16[8192,640]{1,0:T(8,128)(2,1)} async-done(((bf16[256,640]{1,0:T(8,128)(2,1)}), bf16[8192,640]{1,0:T(8,128)(2,1)}) %all-gather.3.cloned.1.call-update) | async-done | bytes 10485776 | tf_op jit(solution)/shard_map/all_gather | solution.py:20
  191.7 6.1 %fusion = f32[192,4096]{1,0:T(8,128)} fusion(bf16[8192,640]{1,0:T(8,128)(2,1)} %all-gather.3.cloned.1.call-done, bf16[192,128]{1,0:T(8,128)(2,1)S(1)} %convolution_convert_fusion.1, bf16[192,512]{1,0:T(8,128)(2,1)S(1)} %fusion.21), kind=kOutput, calls=%fused_computation.1 | convolution fusion | flops 1007124480 | bytes 8634368 | tf_op jit(solution)/shard_map/dot_general | solution.py:10
  197.8 4.7 %fusion.6 = f32[192,640]{1,0:T(8,128)} fusion(bf16[192,4096]{1,0:T(8,128)(2,1)S(1)} %multiply_convert_fusion.1, bf16[8192,640]{1,0:T(8,128)(2,1)} %all-gather.3.cloned.1.call-done), kind=kOutput, calls=%fused_computation.8 | convolution fusion | flops 1006632960 | bytes 7307264 | tf_op jit(solution)/shard_map/dot_general | solution.py:10
  202.5 5.3 %multiply_reduce_fusion.2 = (f32[192]{0:T(256)S(1)}, f32[192]{0:T(256)S(1)}, f32[192,4096]{1,0:T(8,128)S(1)}) fusion(f32[192,4096]{1,0:T(8,128)} %fusion, bf16[8192,512]{0,1:T(8,128)(2,1)} %all-gather.5.cloned.1.call-done, f32[192,640]{1,0:T(8,128)} %fusion.6, bf16[1024,128]{1,0:T(8,128)(2,1)} %all_gather.10, bf16[192,4096]{1,0:T(8,128)(2,1)} %bitcast.29), kind=kOutput, calls=%fused_computation.19 | convolution fusion | flops 836984448 | bytes 12682752 | tf_op jit(solution)/shard_map/dot_general | solution.py:10
  207.8 3.4 %add_convert_fusion.1 = bf16[192,4096]{1,0:T(8,128)(2,1)S(1)} fusion(f32[192,4096]{1,0:T(8,128)} %fusion, f32[192,4096]{1,0:T(8,128)S(1)} %get-tuple-element.5, f32[192]{0:T(256)S(1)} %get-tuple-element.9, f32[192]{0:T(256)S(1)} %get-tuple-element.8, bf16[6,32,4096]{2,1,0:T(8,128)(2,1)} %param.8), kind=kLoop, calls=%fused_computation.17 | loop fusion | flops 6291456 | bytes 9438720 | tf_op jit(solution)/shard_map/convert_element_type | solution.py:64
  211.2 4.3 %fusion.18 = bf16[192,512]{1,0:T(8,128)(2,1)S(1)} fusion(bf16[192,4096]{1,0:T(8,128)(2,1)S(1)} %add_convert_fusion.1, bf16[8192,512]{0,1:T(8,128)(2,1)} %all-gather.5.cloned.1.call-done), kind=kOutput, calls=%fused_computation.30 | convolution fusion | flops 805404672 | bytes 5963776 | tf_op jit(solution)/shard_map/dot_general | solution.py:10
  215.5 0.2 convolution_convert_fusion
  215.8 0.6 copy-done.10
  216.4 2.2 fusion.14
  218.6 2.8 fusion.25
  221.4 3.4 %pad_maximum_fusion = f32[16,288,128]{2,1,0:T(8,128)} fusion(f32[16,32,128]{2,1,0:T(8,128)} %bitcast.35, f32[16,256,128]{2,1,0:T(8,128)} %bitcast.31), kind=kLoop, calls=%fused_computation.24 | loop fusion | flops 589824 | bytes 4718592 | tf_op jit(solution)/shard_map/concatenate | solution.py:81
  224.9 4.6 %multiply_reduce_fusion = (f32[192]{0:T(256)S(1)}, f32[192,4096]{1,0:T(8,128)S(1)}) fusion(bf16[8192,640]{1,0:T(8,128)(2,1)} %all-gather.3.cloned.1.call-done, bf16[192,128]{1,0:T(8,128)(2,1)S(1)} %copy-done.11, bf16[192,512]{1,0:T(8,128)(2,1)S(1)} %fusion.18, bf16[192,4096]{1,0:T(8,128)(2,1)S(1)} %bitcast.30), kind=kOutput, calls=%fused_computation.16 | convolution fusion | flops 1009483584 | bytes 10208000 | tf_op jit(solution)/shard_map/dot_general | solution.py:10
  229.5 1.3 fusion.13
  230.8 1.8 gather_fusion
  232.6 54.1 %reduce-scatter.2.cloned.1.call-done = f32[1,288,128]{2,1,0:T(8,128)} async-done(((f32[16,288,128]{2,1,0:T(8,128)}), f32[1,288,128]{2,1,0:T(8,128)}) %reduce-scatter.2.cloned.1.call-update) | async-done | bytes 147472 | tf_op jit(solution)/shard_map/reduce_scatter | solution.py:84
  286.7 1.6 slice.72
  288.3 1.3 slice_bitcast_fusion
  (37 shorter events, 0.5 us)
Async XLA Ops:
  7.2 51.7 %copy-start = (bf16[6,32,4096]{2,1,0:T(8,128)(2,1)S(1)}, bf16[6,32,4096]{2,1,0:T(8,128)(2,1)}, u32[]{:S(2)}) copy-start(bf16[6,32,4096]{2,1,0:T(8,128)(2,1)} %param.7) | copy-start | bytes 4718596
  7.2 96.7 %all-gather.5.cloned.1.call-start = ((), (), s32[]{:S(2)}) async-start(), calls=%async_computation.2 | async-start | bytes 8650752 | tf_op jit(solution)/shard_map/all_gather | solution.py:20
  7.9 183.8 %all-gather.3.cloned.1.call-start = ((), (), s32[]{:S(2)}) async-start(), calls=%async_computation.1 | async-start | bytes 10813440 | tf_op jit(solution)/shard_map/all_gather | solution.py:20
  9.7 277.0 %reduce-scatter.2.cloned.1.call-start = ((), (), s32[]{:S(2)}) async-start(), calls=%async_computation.3 | async-start | bytes 2506752 | tf_op jit(solution)/shard_map/reduce_scatter | solution.py:84
  59.2 138.5 %copy-start.4 = (bf16[192,4096]{1,0:T(8,128)(2,1)}, bf16[192,4096]{1,0:T(8,128)(2,1)S(1)}, u32[]{:S(2)}) copy-start(bf16[192,4096]{1,0:T(8,128)(2,1)S(1)} %multiply_convert_fusion.1) | copy-start | bytes 4718596
  103.9 4.2 %copy-start.6 = (bf16[1024,128]{1,0:T(8,128)(2,1)S(1)}, bf16[1024,128]{1,0:T(8,128)(2,1)}, u32[]{:S(2)}) copy-start(bf16[1024,128]{1,0:T(8,128)(2,1)} %all_gather.10) | copy-start | bytes 786436
  108.3 89.4 %copy-start.8 = (bf16[192,128]{1,0:T(8,128)(2,1)}, bf16[192,128]{1,0:T(8,128)(2,1)S(1)}, u32[]{:S(2)}) copy-start(bf16[192,128]{1,0:T(8,128)(2,1)S(1)} %convolution_convert_fusion.1) | copy-start | bytes 147460
  211.2 4.4 %copy-start.2 = (bf16[192,4096]{1,0:T(8,128)(2,1)}, bf16[192,4096]{1,0:T(8,128)(2,1)S(1)}, u32[]{:S(2)}) copy-start(bf16[192,4096]{1,0:T(8,128)(2,1)S(1)} %add_convert_fusion.1) | copy-start | bytes 4718596
  211.2 4.4 %copy-start.7 = (bf16[1024,128]{1,0:T(8,128)(2,1)S(1)}, bf16[1024,128]{1,0:T(8,128)(2,1)}, u32[]{:S(2)}) copy-start(bf16[1024,128]{1,0:T(8,128)(2,1)} %all_gather.10) | copy-start | bytes 786436
  211.2 5.2 %copy-start.5 = (bf16[192,4096]{1,0:T(8,128)(2,1)S(1)}, bf16[192,4096]{1,0:T(8,128)(2,1)}, u32[]{:S(2)}) copy-start(bf16[192,4096]{1,0:T(8,128)(2,1)} %copy-done.4) | copy-start | bytes 4718596
  211.2 5.2 %copy-start.9 = (bf16[192,128]{1,0:T(8,128)(2,1)S(1)}, bf16[192,128]{1,0:T(8,128)(2,1)}, u32[]{:S(2)}) copy-start(bf16[192,128]{1,0:T(8,128)(2,1)} %copy-done.8) | copy-start | bytes 147460
  215.8 0.6 copy-start.10
  221.4 3.5 %copy-start.12 = (s32[6]{0:T(128)S(1)}, s32[6]{0:T(128)}, u32[]{:S(2)}) copy-start(s32[6]{0:T(128)} %param.9) | copy-start | bytes 76
  221.4 3.5 %copy-start.1 = (bf16[6,32,4096]{2,1,0:T(8,128)(2,1)S(1)}, bf16[6,32,4096]{2,1,0:T(8,128)(2,1)}, u32[]{:S(2)}) copy-start(bf16[6,32,4096]{2,1,0:T(8,128)(2,1)} %param.7) | copy-start | bytes 4718596
  221.4 3.5 %copy-start.11 = (bf16[192,128]{1,0:T(8,128)(2,1)S(1)}, bf16[192,128]{1,0:T(8,128)(2,1)}, u32[]{:S(2)}) copy-start(bf16[192,128]{1,0:T(8,128)(2,1)} %copy-done.10) | copy-start | bytes 147460
  224.9 4.6 %copy-start.3 = (bf16[192,4096]{1,0:T(8,128)(2,1)S(1)}, bf16[192,4096]{1,0:T(8,128)(2,1)}, u32[]{:S(2)}) copy-start(bf16[192,4096]{1,0:T(8,128)(2,1)} %copy-done.2) | copy-start | bytes 4718596
Sparse Core Ops, SparseCore 0:
  10.9 92.9 all-gather.4
  107.3 84.3 all-gather.2
  225.0 61.7 reduce-scatter.1

commit v2 on v1

--- a/solution.py
+++ b/solution.py
@@ -1,9 +1,173 @@
+import functools
+
 import jax
 import jax.numpy as jnp
 from jax import lax
+from jax.experimental import pallas as pl
+from jax.experimental.pallas import tpu as pltpu
 from jax.sharding import PartitionSpec as P
 
 epsilon = 1e-05
+MESH = pl.DeviceIdType.MESH
+X, Y, Z = 0, 1, 2
+
+
+def plan_of(shapes):
+    half0, half1 = shapes[0][0] // 2, shapes[1][0] // 2
+    return (
+        (0, 0, half0, (Y, Z, X)),
+        (0, half0, half0, (X, Z, Y)),
+        (1, 0, half1, (Z, Y, X)),
+        (1, half1, half1, (Z, X, Y)),
+        (2, 0, shapes[2][0], (Z, Y, X)),
+    )
+
+
+def spread_kernel(lines, plan, a_ref, b_ref, c_ref, a_out, b_out, c_out, own_sem, recv_sem, send_sem):
+    sources, outs = (a_ref, b_ref, c_ref), (a_out, b_out, c_out)
+    fsdp = lines * 4
+    s, f = lax.axis_index("section"), lax.axis_index("fsdp")
+    core, y, z = f % 2, (f // 2) % 2, f // 4
+
+    def place(s_, z_, y_, c_):
+        return {"section": s_, "fsdp": (z_ * 2 + y_) * 2 + c_}
+
+    partner = place(s, z, y, 1 - core)
+    across = place(1 - s, z, y, core)
+    beside = place(s, z, 1 - y, core)
+    above = place(s, z + 1, y, core)
+    below = place(s, z - 1, y, core)
+
+    barrier = pltpu.get_barrier_semaphore()
+    for target in (partner, across, beside):
+        pl.semaphore_signal(barrier, inc=1, device_id=target, device_id_type=MESH)
+
+    @pl.when(z + 1 < lines)
+    def _():
+        pl.semaphore_signal(barrier, inc=1, device_id=above, device_id_type=MESH)
+
+    @pl.when(z > 0)
+    def _():
+        pl.semaphore_signal(barrier, inc=1, device_id=below, device_id_type=MESH)
+
+    ends = (z + 1 < lines).astype(jnp.int32) + (z > 0).astype(jnp.int32)
+    pl.semaphore_wait(barrier, 3 + ends)
+
+    def when(test, action):
+        if test is True:
+            action()
+        else:
+            pl.when(test)(action)
+
+    def both(left, right):
+        return right if left is True else left if right is True else left & right
+
+    def slot_of(dx, dy, dz, c_):
+        return ((s + dx) % 2) * fsdp + ((z + dz) * 2 + (y + dy) % 2) * 2 + c_
+
+    def piece(index, slot):
+        array, first, rows, _ = plan[index]
+        return outs[array].at[slot, pl.ds(first, rows)]
+
+    def sends(index, dx, dy, dz, step):
+        array, first, rows, order = plan[index]
+        slot = slot_of(dx, dy, dz, core)
+        own = dx == 0 and dy == 0 and dz == 0
+        source = sources[array].at[pl.ds(first, rows)] if own else piece(index, slot)
+        gone = {X: dx != 0, Y: dy != 0, Z: dz != 0}
+        result = []
+
+        def add(way, test, target):
+            copy = pltpu.make_async_remote_copy(
+                src_ref=source,
+                dst_ref=piece(index, slot),
+                send_sem=send_sem.at[step * 5 + way],
+                recv_sem=recv_sem.at[slot * len(plan) + index],
+                device_id=target,
+                device_id_type=MESH,
+            )
+            result.append((test, copy))
+
+        for rank, dim in enumerate(order):
+            if any(gone[later] for later in order[rank + 1:]):
+                continue
+            if dim == Z:
+                if dz <= 0:
+                    add(0, z + 1 < lines, above)
+                if dz >= 0:
+                    add(1, z > 0, below)
+            elif not gone[dim]:
+                add(2 + dim, True, across if dim == X else beside)
+        add(4, True, partner)
+        return result
+
+    events = []
+    for dx in (0, 1):
+        for dy in (0, 1):
+            for dz in range(1 - lines, lines):
+                for index in range(len(plan)):
+                    events.append((dx + dy + abs(dz), index, dx, dy, dz))
+    events.sort(key=lambda event: (event[0], abs(event[4]), event[1]))
+    steps = {}
+
+    def step_of(index, dx, dy, dz):
+        return steps.setdefault((index, dx, dy, dz % lines), len(steps))
+
+    def inside(dz):
+        return True if dz == 0 else (z + dz < lines) if dz > 0 else (z + dz >= 0)
+
+    copies = []
+    for array in range(3):
+        copy = pltpu.make_async_copy(sources[array], outs[array].at[slot_of(0, 0, 0, core)], own_sem.at[array])
+        copy.start()
+        copies.append(copy)
+
+    def arrival(index, slot):
+        ref = piece(index, slot)
+        sem = recv_sem.at[slot * len(plan) + index]
+        pltpu.make_async_copy(ref, ref, sem).wait()
+
+    def run(event):
+        distance, index, dx, dy, dz = event
+        step = step_of(index, dx, dy, dz)
+
+        def action():
+            if distance:
+                arrival(index, slot_of(dx, dy, dz, core))
+            for test, copy in sends(index, dx, dy, dz, step):
+                when(test, copy.start)
+
+        when(inside(dz), action)
+
+    for event in events:
+        run(event)
+    for _, index, dx, dy, dz in events:
+        when(inside(dz), functools.partial(arrival, index, slot_of(dx, dy, dz, 1 - core)))
+    for copy in copies:
+        copy.wait()
+    for _, index, dx, dy, dz in events:
+        for test, copy in sends(index, dx, dy, dz, step_of(index, dx, dy, dz)):
+            when(both(inside(dz), test), copy.wait_send)
+
+
+def spread(joined, proj, up):
+    fsdp = lax.axis_size("fsdp")
+    devices = fsdp * lax.axis_size("section")
+    blocks = (joined, proj, up)
+    plan = plan_of([block.shape for block in blocks])
+    pieces = len(plan)
+    return pl.pallas_call(
+        functools.partial(spread_kernel, fsdp // 4, plan),
+        out_shape=[jax.ShapeDtypeStruct((devices,) + b.shape, b.dtype) for b in blocks],
+        in_specs=[pl.BlockSpec(memory_space=pltpu.VMEM)] * 3,
+        out_specs=[pl.BlockSpec(memory_space=pl.ANY)] * 3,
+        scratch_shapes=[
+            pltpu.SemaphoreType.DMA((3,)),
+            pltpu.SemaphoreType.DMA((devices * pieces,)),
+            pltpu.SemaphoreType.DMA((fsdp * pieces * 5,)),
+        ],
+        compiler_params=pltpu.CompilerParams(collective_id=0, has_side_effects=True),
+    )(*blocks)
 
 
 def widen_dot(left, right, dims=((1,), (0,))):
@@ -15,6 +179,12 @@
     joined = jnp.concatenate([w_value[0], adapter_down[0]], axis=1)
     proj = w_out[0].T
     up = adapter_up[0].T
+
+    fsdp = lax.axis_size("fsdp")
+    if sections == 2 and fsdp % 4 == 0 and fsdp <= 16:
+        return tuple(
+            full.reshape(sections, -1, full.shape[2]) for full in spread(joined, proj, up)
+        )
 
     def whole(block):
         full = lax.all_gather(block, ("section", "fsdp"), axis=0, tiled=True)

time: 296 us -> 213 us (0.72)
  waiting for transfers between devices: 183 us -> 52.4 us
  Pallas kernels: 0 us -> 80.6 us
  blocking collectives: 47.2 us -> 0 us
  local copies, waits for them, and re-layouts: 5.48 us -> 25 us
  matrix products: 34.6 us -> 28 us
    all_gather x2 -> x0, waiting for transfers between devices: 128 us -> none  [whole(): full = lax.all_gather(block, ('section', 'fsdp'), axis=0, tiled=True)]
    pallas_call x0 -> x1, Pallas kernels: none -> 80.6 us  [spread(): pl.pallas_call(functools.partial(spread_kernel, fsdp // 4, plan), out_sha...]
    all_gather x1 -> x0, blocking collectives: 47.2 us -> none  [whole(): full = lax.all_gather(block, ('section', 'fsdp'), axis=0, tiled=True)]
    slice x0 -> x3, local copies, waits for them, and re-layouts: none -> 16.3 us  [the longest x1 9.55 us: body(): both = widen_dot(normed, joined[layer])]
    dot_general x10, matrix products: 34.6 us -> 28 us  [widen_dot(): lax.dot_general(left, right, (dims, ((), ())), preferred_element_type=jnp...]
  transfers between devices with their start and end apart: 3 -> 1, of which waited for: 3 -> 1; matrix products, arithmetic and copies ran while one was open for 5% -> 5% of each run, Pallas kernels for 0% -> 0%
where the time goes in v2:
time: 213 us
  Pallas kernels  80.6 us (38%)
  waiting for transfers between devices  52.4 us (25%)
  matrix products  28 us (13%)
  local copies, waits for them, and re-layouts  25 us (12%)
  between operations  14.2 us (7%)
  other arithmetic  12.9 us (6%)
    pallas_call x1, Pallas kernels, spread(): pl.pallas_call(functools.partial(spread_kernel, fsdp // 4, plan), out_sha...  80.6 us
    reduce_scatter x1, waiting for transfers between devices, body(): lax.psum_scatter(parts, 'fsdp', scatter_dimension=0, tiled=True)[0]  52.3 us
    dot_general x10, matrix products, widen_dot(): lax.dot_general(left, right, (dims, ((), ())), preferred_element_type=jnp...  28 us
    slice x1, local copies, waits for them, and re-layouts, body(): both = widen_dot(normed, joined[layer])  9.55 us
    slice x1, local copies, waits for them, and re-layouts, body(): proj[layer]  6.08 us
    convert_element_type x1, other arithmetic, body(): upstream = (upstream.astype(jnp.float32) + inverse * (d_normed - widened...  4.42 us
  transfers between devices with their start and end apart: 1, of which 1 were waited for; matrix products, arithmetic and copies ran while one was open for 5% of the time, Pallas kernels for 0%

profile of v2, /device:TPU:0, one launch (start us, length us, event | category | flops | bytes accessed | tf_op | source)
XLA Modules:
  0.0 213.1 jit_solution(9445192070772325625)
XLA Ops:
  7.2 1.8 multiply_reduce_fusion.3
  9.1 1.8 multiply_convert_fusion
  11.0 0.8 copy.10
  11.8 0.8 pad_maximum_fusion.1.a_ref
  12.6 80.6 %shard_map.94 = (bf16[32,256,640]{2,1,0:T(8,128)(2,1)}, bf16[32,256,512]{2,1,0:T(8,128)(2,1)}, bf16[32,32,128]{2,1,0:T(8,128)(2,1)}) custom-call(bf16[256,640]{1,0:T(8,128)(2,1)} %pad_maximum_fusion.1.a_ref, bf16[256,512]{1,0:T(8,128)(2,1)} %bitcast.68, bf16[32,128]{1,0:T(8,128)(2,1)} %bitcast.72), custom_call_target="tpu_custom_call" | custom-call | tf_op jit(solution)/shard_map/pallas_call | solution.py:159
  93.2 6.1 %fusion.31 = (bf16[16,256,512]{2,1,0:T(8,128)(2,1)}, bf16[16,256,512]{2,1,0:T(8,128)(2,1)}) fusion(bf16[32,256,512]{2,1,0:T(8,128)(2,1)} %get-tuple-element.8), kind=kLoop, calls=%fused_computation.56 | loop fusion | bytes 16777216 | tf_op jit(solution)/shard_map/slice | solution.py:218
  99.9 9.6 %fusion.30 = (bf16[16,256,640]{2,1,0:T(8,128)(2,1)}, bf16[16,256,640]{2,1,0:T(8,128)(2,1)}) fusion(bf16[32,256,640]{2,1,0:T(8,128)(2,1)} %get-tuple-element.6), kind=kLoop, calls=%fused_computation.55 | loop fusion | bytes 20971520 | tf_op jit(solution)/shard_map/slice | solution.py:213
  109.5 3.3 %convolution_convert_fusion = bf16[512,192]{0,1:T(8,128)(2,1)S(1)} fusion(bf16[192,4096]{1,0:T(8,128)(2,1)S(1)} %bitcast.63, bf16[4096,512]{1,0:T(8,128)(2,1)} %bitcast.61), kind=kOutput, calls=%fused_computation.21 | convolution fusion | flops 805404672 | bytes 5963776 | tf_op jit(solution)/shard_map/dot_general | solution.py:174
  113.3 1.4 fusion.34
  114.8 1.2 copy-done.2
  116.0 3.6 %fusion.14 = f32[192,4096]{1,0:T(8,128)} fusion(bf16[4096,640]{1,0:T(8,128)(2,1)S(1)} %bitcast.55, bf16[192,128]{1,0:T(8,128)(2,1)S(1)} %convolution_convert_fusion.3, bf16[192,512]{1,0:T(8,128)(2,1)S(1)} %bitcast.62), kind=kOutput, calls=%fused_computation.31 | convolution fusion | flops 1007124480 | bytes 8634368 | tf_op jit(solution)/shard_map/dot_general | solution.py:174
  119.6 6.5 %multiply_reduce_fusion.2 = (f32[192]{0:T(256)S(1)}, f32[192]{0:T(256)S(1)}, f32[192,4096]{1,0:T(8,128)}) fusion(f32[192,4096]{1,0:T(8,128)} %fusion.14, bf16[4096,512]{1,0:T(8,128)(2,1)} %bitcast.56, bf16[512,128]{1,0:T(8,128)(2,1)S(1)} %bitcast.65, f32[192,640]{1,0:T(8,128)S(1)} %fusion.34, bf16[192,4096]{1,0:T(8,128)(2,1)S(1)} %bitcast.49), kind=kOutput, calls=%fused_computation.8 | convolution fusion | flops 836984448 | bytes 12682752 | tf_op jit(solution)/shard_map/dot_general | solution.py:174
  126.1 4.4 %add_convert_fusion.1 = bf16[192,4096]{1,0:T(8,128)(2,1)S(1)} fusion(f32[192,4096]{1,0:T(8,128)} %fusion.14, f32[192,4096]{1,0:T(8,128)} %get-tuple-element.17, f32[192]{0:T(256)S(1)} %get-tuple-element.21, f32[192]{0:T(256)S(1)} %get-tuple-element.20, bf16[6,32,4096]{2,1,0:T(8,128)(2,1)} %param.8), kind=kLoop, calls=%fused_computation.6 | loop fusion | flops 6291456 | bytes 9438720 | tf_op jit(solution)/shard_map/convert_element_type | solution.py:234
  130.6 1.0 convolution_convert_fusion.1
  131.6 0.8 convolution_convert_fusion.2
  132.5 3.8 %fusion.10 = f32[512,128]{1,0:T(8,128)} fusion(bf16[4096,640]{1,0:T(8,128)(2,1)} %bitcast.54, bf16[192,512]{1,0:T(8,128)(2,1)S(1)} %convolution_convert_fusion.1, pred[]{:T(512)S(6)} %eq.2, f32[192,640]{1,0:T(8,128)} %copy-done.8, bf16[512,192]{0,1:T(8,128)(2,1)S(1)} %convolution_convert_fusion, f32[192,4096]{1,0:T(8,128)} %get-tuple-element.17, ...), kind=kOutput, calls=%fused_computation.27 | convolution fusion | flops 228212736 | bytes 4900608 | tf_op jit(solution)/shard_map/dot_general | solution.py:174
  136.2 2.9 %fusion.4 = f32[4096,128]{1,0:T(8,128)S(1)} fusion(f32[192]{0:T(256)S(1)} %rsqrt.22, pred[]{:T(512)S(6)} %eq.2, bf16[192,128]{1,0:T(8,128)(2,1)} %copy-done.10, bf16[192,128]{1,0:T(8,128)(2,1)} %convolution_convert_fusion.2, f32[192,4096]{1,0:T(8,128)} %get-tuple-element.17, f32[192]{0:T(256)S(1)} %get-tuple-element.20, bf16[192,4096]{1,0:T(8,128)(2,1)S(1)} %bitcast.50), kind=kOutput, calls=%fused_computation.16 | convolution fusion | flops 206069760 | bytes 6915585 | tf_op jit(solution)/shard_map/dot_general | solution.py:174
  139.1 1.6 pad_maximum_fusion
  140.8 4.5 %multiply_reduce_fusion = (f32[192]{0:T(256)S(1)}, f32[192,4096]{1,0:T(8,128)S(1)}) fusion(bf16[4096,640]{1,0:T(8,128)(2,1)} %bitcast.52, bf16[192,128]{1,0:T(8,128)(2,1)S(1)} %copy-done.11, bf16[192,512]{1,0:T(8,128)(2,1)S(1)} %convolution_convert_fusion.1, bf16[192,4096]{1,0:T(8,128)(2,1)S(1)} %bitcast.51), kind=kOutput, calls=%fused_computation.5 | convolution fusion | flops 1009483584 | bytes 10208000 | tf_op jit(solution)/shard_map/dot_general | solution.py:174
  145.3 2.4 %fusion.2 = bf16[192,4096]{1,0:T(8,128)(2,1)} fusion(bf16[192,4096]{1,0:T(8,128)(2,1)S(1)} %add_convert_fusion.1, f32[192,4096]{1,0:T(8,128)S(1)} %get-tuple-element.19, f32[192]{0:T(256)S(1)} %broadcast_multiply_fusion, f32[192]{0:T(256)S(1)} %rsqrt.22, pred[]{:T(512)S(6)} %eq.2, bf16[6,32,4096]{2,1,0:T(8,128)(2,1)S(1)} %copy-done), kind=kLoop, calls=%fused_computation.13 | loop fusion | flops 7864320 | bytes 7865857 | tf_op jit(solution)/shard_map/jit(_where)/select_n | solution.py:242
  147.7 3.3 %gather_fusion = bf16[6,32,4096]{2,1,0:T(8,128)(2,1)} fusion(bf16[6,32,4096]{2,1,0:T(8,128)(2,1)} %bitcast.60, s32[1024]{0:T(1024)S(1)} %pad_clamp_fusion), kind=kCustom, calls=%fused_computation | custom fusion | bytes 3145752 | tf_op jit(solution)/shard_map/gather | solution.py:256
  151.0 52.3 %reduce-scatter.2.cloned.1.call-done = f32[1,288,128]{2,1,0:T(8,128)} async-done(((f32[16,288,128]{2,1,0:T(8,128)}), f32[1,288,128]{2,1,0:T(8,128)}) %reduce-scatter.2.cloned.1.call-update) | async-done | bytes 147472 | tf_op jit(solution)/shard_map/reduce_scatter | solution.py:254
  203.4 1.6 slice.65
  204.9 1.3 slice_bitcast_fusion
  (43 shorter events, 1.4 us)
Async XLA Ops:
  7.2 3.8 %copy-start.12 = (bf16[1,512,256]{2,1,0:T(8,128)(2,1)S(1)}, bf16[1,512,256]{2,1,0:T(8,128)(2,1)}, u32[]{:S(2)}) copy-start(bf16[1,512,256]{2,1,0:T(8,128)(2,1)} %param.11) | copy-start | bytes 786436
  7.2 4.6 %copy-start.13 = (bf16[1,256,512]{2,1,0:T(8,128)(2,1)S(1)}, bf16[1,256,512]{2,1,0:T(8,128)(2,1)}, u32[]{:S(2)}) copy-start(bf16[1,256,512]{2,1,0:T(8,128)(2,1)} %param.10) | copy-start | bytes 786436
  7.2 4.6 %copy-start.15 = (bf16[1,256,128]{2,1,0:T(8,128)(2,1)S(1)}, bf16[1,256,128]{2,1,0:T(8,128)(2,1)}, u32[]{:S(2)}) copy-start(bf16[1,256,128]{2,1,0:T(8,128)(2,1)} %param.12) | copy-start | bytes 196612
  7.2 196.2 %reduce-scatter.2.cloned.1.call-start = ((), (), s32[]{:S(2)}) async-start(), calls=%async_computation.1 | async-start | bytes 2506752 | tf_op jit(solution)/shard_map/reduce_scatter | solution.py:254
  93.2 6.1 %copy-start.14 = (bf16[32,32,128]{2,1,0:T(8,128)(2,1)S(1)}, bf16[32,32,128]{2,1,0:T(8,128)(2,1)}, u32[]{:S(2)}) copy-start(bf16[32,32,128]{2,1,0:T(8,128)(2,1)} %get-tuple-element.7) | copy-start | bytes 786436
  99.9 19.7 %copy-start.5 = (bf16[16,32,128]{2,1,0:T(8,128)(2,1)}, bf16[16,32,128]{2,1,0:T(8,128)(2,1)S(1)}, u32[]{:S(2)}) copy-start(bf16[16,32,128]{2,1,0:T(8,128)(2,1)S(1)} %get-tuple-element.15) | copy-start | bytes 393220
  99.9 9.6 %copy-start.4 = (bf16[6,32,4096]{2,1,0:T(8,128)(2,1)S(1)}, bf16[6,32,4096]{2,1,0:T(8,128)(2,1)}, u32[]{:S(2)}) copy-start(bf16[6,32,4096]{2,1,0:T(8,128)(2,1)} %param.8) | copy-start | bytes 4718596
  109.5 3.3 %copy-start.9 = (bf16[16,32,128]{2,1,0:T(8,128)(2,1)S(1)}, bf16[16,32,128]{2,1,0:T(8,128)(2,1)}, u32[]{:S(2)}) copy-start(bf16[16,32,128]{2,1,0:T(8,128)(2,1)} %get-tuple-element.16) | copy-start | bytes 393220
  109.5 3.8 %copy-start.1 = (bf16[16,256,640]{2,1,0:T(8,128)(2,1)S(1)}, bf16[16,256,640]{2,1,0:T(8,128)(2,1)}, u32[]{:S(2)}) copy-start(bf16[16,256,640]{2,1,0:T(8,128)(2,1)} %get-tuple-element.11) | copy-start | bytes 15728644
  113.0 1.8 copy-start.10
  113.3 2.7 %copy-start.2 = (bf16[16,256,640]{2,1,0:T(8,128)(2,1)S(1)}, bf16[16,256,640]{2,1,0:T(8,128)(2,1)}, u32[]{:S(2)}) copy-start(bf16[16,256,640]{2,1,0:T(8,128)(2,1)} %get-tuple-element.12) | copy-start | bytes 15728644
  114.8 4.8 %copy-start.8 = (f32[192,640]{1,0:T(8,128)}, f32[192,640]{1,0:T(8,128)S(1)}, u32[]{:S(2)}) copy-start(f32[192,640]{1,0:T(8,128)S(1)} %fusion.34) | copy-start | bytes 1474564
  116.0 3.6 %copy-start = (bf16[6,32,4096]{2,1,0:T(8,128)(2,1)S(1)}, bf16[6,32,4096]{2,1,0:T(8,128)(2,1)}, u32[]{:S(2)}) copy-start(bf16[6,32,4096]{2,1,0:T(8,128)(2,1)} %param.7) | copy-start | bytes 4718596
  126.1 4.5 %copy-start.3 = (bf16[16,256,512]{2,1,0:T(8,128)(2,1)S(1)}, bf16[16,256,512]{2,1,0:T(8,128)(2,1)}, u32[]{:S(2)}) copy-start(bf16[16,256,512]{2,1,0:T(8,128)(2,1)} %get-tuple-element.13) | copy-start | bytes 12582916
  130.6 1.0 copy-start.6
  136.2 2.9 %copy-start.7 = (f32[512,128]{1,0:T(8,128)S(1)}, f32[512,128]{1,0:T(8,128)}, u32[]{:S(2)}) copy-start(f32[512,128]{1,0:T(8,128)} %fusion.10) | copy-start | bytes 786436
  139.1 1.6 copy-start.16
  139.1 1.7 copy-start.11
Sparse Core Ops, SparseCore 0:
  140.9 62.4 reduce-scatter.1

commit v3 on v2

--- a/solution.py
+++ b/solution.py
@@ -170,8 +170,83 @@
     )(*blocks)
 
 
+def settle_kernel(parts_ref, down_ref, up_ref, near, mine, far, near_send, near_recv, far_send, far_recv):
+    chips = parts_ref.shape[0]
+    f = lax.axis_index("fsdp")
+    core, chip = f % 2, f // 2
+    barrier = pltpu.get_barrier_semaphore()
+    pl.semaphore_signal(barrier, inc=1, device_id={"fsdp": chip * 2 + 1 - core}, device_id_type=MESH)
+    for step in range(1, chips):
+        other = (chip + step) % chips
+        pl.semaphore_signal(barrier, inc=1, device_id={"fsdp": other * 2 + core}, device_id_type=MESH)
+    pl.semaphore_wait(barrier, chips)
+
+    handed, passed = [], []
+    for step in range(chips):
+        other = (chip + 1 + step) % chips
+        copy = pltpu.make_async_remote_copy(
+            src_ref=parts_ref.at[other, 1 - core],
+            dst_ref=near.at[step],
+            send_sem=near_send.at[step],
+            recv_sem=near_recv.at[step],
+            device_id={"fsdp": chip * 2 + 1 - core},
+            device_id_type=MESH,
+        )
+        copy.start()
+        handed.append(copy)
+    for step in range(chips - 1):
+        other = (chip + 1 + step) % chips
+        handed[step].wait_recv()
+        mine[step] = (
+            parts_ref[other, core].astype(jnp.float32) + near[step].astype(jnp.float32)
+        ).astype(mine.dtype)
+        copy = pltpu.make_async_remote_copy(
+            src_ref=mine.at[step],
+            dst_ref=far.at[step],
+            send_sem=far_send.at[step],
+            recv_sem=far_recv.at[step],
+            device_id={"fsdp": other * 2 + core},
+            device_id_type=MESH,
+        )
+        passed.append(copy)
+        if step:
+            passed[step - 1].start()
+    handed[-1].wait_recv()
+    total = parts_ref[chip, core].astype(jnp.float32) + near[chips - 1].astype(jnp.float32)
+    passed[-1].start()
+    for step in range(chips - 1):
+        passed[step].wait_recv()
+        total = total + far[step].astype(jnp.float32)
+    split = down_ref.shape[0]
+    down_ref[...] = total[:split]
+    up_ref[...] = total[split:]
+    for copy in handed + passed:
+        copy.wait_send()
+
+
+def settle(parts, split):
+    chips, _, rows, rank = parts.shape
+    buffer = pltpu.VMEM((chips, rows, rank), parts.dtype)
+    return pl.pallas_call(
+        settle_kernel,
+        out_shape=[
+            jax.ShapeDtypeStruct((split, rank), jnp.float32),
+            jax.ShapeDtypeStruct((rows - split, rank), jnp.float32),
+        ],
+        in_specs=[pl.BlockSpec(memory_space=pltpu.VMEM)],
+        out_specs=[pl.BlockSpec(memory_space=pltpu.VMEM)] * 2,
+        scratch_shapes=[buffer, buffer, buffer] + [pltpu.SemaphoreType.DMA((chips,))] * 4,
+        compiler_params=pltpu.CompilerParams(collective_id=1, has_side_effects=True),
+    )(parts)
+
+
 def widen_dot(left, right, dims=((1,), (0,))):
     return lax.dot_general(left, right, (dims, ((), ())), preferred_element_type=jnp.float32)
+
+
+def custom_route():
+    fsdp = lax.axis_size("fsdp")
+    return lax.axis_size("section") == 2 and fsdp % 4 == 0 and fsdp <= 16
 
 
 def gather_weights(w_value, w_out, adapter_down, adapter_up):
@@ -180,8 +255,7 @@
     proj = w_out[0].T
     up = adapter_up[0].T
 
-    fsdp = lax.axis_size("fsdp")
-    if sections == 2 and fsdp % 4 == 0 and fsdp <= 16:
+    if custom_route():
         return tuple(
             full.reshape(sections, -1, full.shape[2]) for full in spread(joined, proj, up)
         )
@@ -251,10 +325,15 @@
     parts = jnp.concatenate(
         [part_down.reshape(shares, -1, rank), part_up.reshape(shares, -1, rank)], axis=1
     )
-    combined = lax.psum_scatter(parts, "fsdp", scatter_dimension=0, tiled=True)[0]
     share_down = features // shares
+    if custom_route():
+        split = parts.astype(jnp.bfloat16).reshape(shares // 2, 2, *parts.shape[1:])
+        grad_down, grad_up = settle(split, share_down)
+    else:
+        combined = lax.psum_scatter(parts, "fsdp", scatter_dimension=0, tiled=True)[0]
+        grad_down, grad_up = combined[:share_down], combined[share_down:]
     out = mine(grads).reshape(micro, local, features)[order]
-    return (out[None], combined[:share_down][None], combined[share_down:].T[None])
+    return (out[None], grad_down[None], grad_up.T[None])
 
 
 def solution(mesh):

time: 213 us -> 162 us (0.76)
  waiting for transfers between devices: 52.4 us -> 0 us
  Pallas kernels: 80.6 us -> 97.8 us
  between operations: 14.2 us -> 0.84 us
  local copies, waits for them, and re-layouts: 25 us -> 21.2 us
    reduce_scatter x1 -> x0, waiting for transfers between devices: 52.3 us -> none  [body(): lax.psum_scatter(parts, 'fsdp', scatter_dimension=0, tiled=True)[0]]
    pallas_call x0 -> x1, Pallas kernels: none -> 17.2 us  [settle(): pl.pallas_call(settle_kernel, out_shape=[jax.ShapeDtypeStruct((split, ran...]
  transfers between devices with their start and end apart: 1 -> 0, of which waited for: 1 -> 0; matrix products, arithmetic and copies ran while one was open for 5% -> 0% of each run, Pallas kernels for 0% -> 0%
where the time goes in v3:
time: 162 us; the launch traced here: 161 us
  Pallas kernels  97.8 us (60%)
  matrix products  29.4 us (18%)
  local copies, waits for them, and re-layouts  21.2 us (13%)
  other arithmetic  11.8 us (7%)
    pallas_call x1, Pallas kernels, spread(): pl.pallas_call(functools.partial(spread_kernel, fsdp // 4, plan), out_sha...  80.6 us
    dot_general x10, matrix products, widen_dot(): lax.dot_general(left, right, (dims, ((), ())), preferred_element_type=jnp...  29.4 us
    pallas_call x1, Pallas kernels, settle(): pl.pallas_call(settle_kernel, out_shape=[jax.ShapeDtypeStruct((split, ran...  17.2 us
    slice x1, local copies, waits for them, and re-layouts, body(): both = widen_dot(normed, joined[layer])  9.47 us
    slice x1, local copies, waits for them, and re-layouts, body(): proj[layer]  5.19 us
    convert_element_type x1, other arithmetic, body(): upstream = (upstream.astype(jnp.float32) + inverse * (d_normed - widened...  4.42 us
    gather x1, local copies, waits for them, and re-layouts, body(): out = mine(grads).reshape(micro, local, features)[order]  3.29 us

profile of v3, /device:TPU:0, one launch (start us, length us, event | category | flops | bytes accessed | tf_op | source)
XLA Modules:
  0.0 161.1 jit_solution(4860841138611873054)
XLA Ops:
  0.6 1.7 %pad_maximum_fusion.1.a_ref = bf16[256,640]{1,0:T(8,128)(2,1)} fusion(bf16[256,128]{1,0:T(8,128)(2,1)} %bitcast.72, bf16[256,512]{1,0:T(8,128)(2,1)} %bitcast.70), kind=kLoop, calls=%fused_computation.30 | loop fusion | flops 655360 | bytes 655360 | tf_op jit(solution)/shard_map/concatenate | solution.py:254
  2.4 1.8 %copy.10 = bf16[1,512,256]{1,2,0:T(8,128)(2,1)} copy(bf16[1,512,256]{2,1,0:T(8,128)(2,1)} %param.11) | data formatting | bytes 524288 | tf_op args[4]
  4.2 80.6 %shard_map.94 = (bf16[32,256,640]{2,1,0:T(8,128)(2,1)}, bf16[32,256,512]{2,1,0:T(8,128)(2,1)}, bf16[32,32,128]{2,1,0:T(8,128)(2,1)}) custom-call(bf16[256,640]{1,0:T(8,128)(2,1)} %pad_maximum_fusion.1.a_ref, bf16[256,512]{1,0:T(8,128)(2,1)} %bitcast.67, bf16[32,128]{1,0:T(8,128)(2,1)} %bitcast.74), custom_call_target="tpu_custom_call" | custom-call | tf_op jit(solution)/shard_map/pallas_call | solution.py:159
  84.8 5.2 %fusion.29 = (bf16[16,256,512]{2,1,0:T(8,128)(2,1)}, bf16[16,256,512]{2,1,0:T(8,128)(2,1)S(1)}) fusion(bf16[32,256,512]{2,1,0:T(8,128)(2,1)} %get-tuple-element.10), kind=kLoop, calls=%fused_computation.55 | loop fusion | bytes 16777216 | tf_op jit(solution)/shard_map/slice | solution.py:292
  90.0 1.0 convolution_convert_fusion.1
  91.0 0.2 convolution_convert_fusion.5
  91.3 9.5 %fusion.28 = (bf16[16,256,640]{2,1,0:T(8,128)(2,1)}, bf16[16,256,640]{2,1,0:T(8,128)(2,1)}) fusion(bf16[32,256,640]{2,1,0:T(8,128)(2,1)} %get-tuple-element.8), kind=kLoop, calls=%fused_computation.54 | loop fusion | bytes 20971520 | tf_op jit(solution)/shard_map/slice | solution.py:287
  100.7 6.2 %fusion.12 = f32[192,4096]{1,0:T(8,128)} fusion(bf16[4096,640]{1,0:T(8,128)(2,1)} %bitcast.54, bf16[192,128]{1,0:T(8,128)(2,1)S(1)} %convolution_convert_fusion.5, bf16[192,512]{1,0:T(8,128)(2,1)S(1)} %bitcast.62), kind=kOutput, calls=%fused_computation.31 | convolution fusion | flops 1007124480 | bytes 8634368 | tf_op jit(solution)/shard_map/dot_general | solution.py:244
  107.0 0.4 multiply_reduce_fusion.3
  107.4 0.4 multiply_convert_fusion
  107.8 1.4 fusion.32
  109.3 6.7 %multiply_reduce_fusion.2 = (f32[192]{0:T(256)S(1)}, f32[192]{0:T(256)S(1)}, f32[192,4096]{1,0:T(8,128)}) fusion(f32[192,4096]{1,0:T(8,128)} %fusion.12, bf16[4096,512]{1,0:T(8,128)(2,1)} %bitcast.56, bf16[512,128]{1,0:T(8,128)(2,1)S(1)} %bitcast.65, f32[192,640]{1,0:T(8,128)S(1)} %fusion.32, bf16[192,4096]{1,0:T(8,128)(2,1)S(1)} %bitcast.47), kind=kOutput, calls=%fused_computation.9 | convolution fusion | flops 836984448 | bytes 12682752 | tf_op jit(solution)/shard_map/dot_general | solution.py:244
  116.0 4.4 %add_convert_fusion.1 = bf16[192,4096]{1,0:T(8,128)(2,1)S(1)} fusion(f32[192,4096]{1,0:T(8,128)} %fusion.12, f32[192,4096]{1,0:T(8,128)} %get-tuple-element.21, f32[192]{0:T(256)S(1)} %get-tuple-element.25, f32[192]{0:T(256)S(1)} %get-tuple-element.24, bf16[6,32,4096]{2,1,0:T(8,128)(2,1)} %param.8), kind=kLoop, calls=%fused_computation.7 | loop fusion | flops 6291456 | bytes 9438720 | tf_op jit(solution)/shard_map/convert_element_type | solution.py:308
  120.4 1.0 convolution_convert_fusion.2
  121.5 0.8 convolution_convert_fusion.4
  122.4 3.8 %convolution_convert_fusion = bf16[4096,128]{1,0:T(8,128)(2,1)} fusion(f32[192]{0:T(256)S(1)} %rsqrt.22, pred[]{:T(512)S(6)} %eq.2, bf16[192,128]{1,0:T(8,128)(2,1)} %copy-done.6, bf16[192,128]{1,0:T(8,128)(2,1)} %convolution_convert_fusion.4, f32[192,4096]{1,0:T(8,128)} %get-tuple-element.21, f32[192]{0:T(256)S(1)} %get-tuple-element.24, ...), kind=kOutput, calls=%fused_computation.4 | convolution fusion | flops 206594048 | bytes 5867009 | tf_op jit(solution)/shard_map/dot_general | solution.py:244
  126.2 3.7 %convolution_convert_fusion.3 = bf16[512,128]{1,0:T(8,128)(2,1)} fusion(bf16[4096,640]{1,0:T(8,128)(2,1)} %bitcast.55, bf16[192,512]{1,0:T(8,128)(2,1)S(1)} %convolution_convert_fusion.2, pred[]{:T(512)S(6)} %eq.2, f32[192,640]{1,0:T(8,128)} %copy-done.5, bf16[512,192]{0,1:T(8,128)(2,1)S(1)} %convolution_convert_fusion.1, ...), kind=kOutput, calls=%fused_computation.23 | convolution fusion | flops 228278272 | bytes 4769536 | tf_op jit(solution)/shard_map/dot_general | solution.py:244
  129.9 2.4 %pad_maximum_fusion.parts_ref = bf16[8,2,288,128]{3,2,1,0:T(8,128)(2,1)} fusion(bf16[8,2,32,128]{3,2,1,0:T(8,128)(2,1)} %bitcast.68, bf16[8,2,256,128]{3,2,1,0:T(8,128)(2,1)} %bitcast.60), kind=kLoop, calls=%fused_computation.19 | loop fusion | flops 2359296 | bytes 2359296 | tf_op jit(solution)/shard_map/concatenate | solution.py:325
  132.3 17.2 %shard_map.95 = (f32[256,128]{1,0:T(8,128)}, f32[32,128]{1,0:T(8,128)}) custom-call(bf16[8,2,288,128]{3,2,1,0:T(8,128)(2,1)} %pad_maximum_fusion.parts_ref), custom_call_target="tpu_custom_call" | custom-call | tf_op jit(solution)/shard_map/pallas_call | solution.py:230
  149.5 4.5 %multiply_reduce_fusion = (f32[192]{0:T(256)S(1)}, f32[192,4096]{1,0:T(8,128)S(1)}) fusion(bf16[4096,640]{1,0:T(8,128)(2,1)} %bitcast.50, bf16[192,128]{1,0:T(8,128)(2,1)S(1)} %copy-done.7, bf16[192,512]{1,0:T(8,128)(2,1)S(1)} %convolution_convert_fusion.2, bf16[192,4096]{1,0:T(8,128)(2,1)S(1)} %bitcast.49), kind=kOutput, calls=%fused_computation.6 | convolution fusion | flops 1009483584 | bytes 10208000 | tf_op jit(solution)/shard_map/dot_general | solution.py:244
  154.1 2.5 %fusion.2 = bf16[192,4096]{1,0:T(8,128)(2,1)} fusion(bf16[192,4096]{1,0:T(8,128)(2,1)S(1)} %add_convert_fusion.1, f32[192,4096]{1,0:T(8,128)S(1)} %get-tuple-element.23, f32[192]{0:T(256)S(1)} %broadcast_multiply_fusion, f32[192]{0:T(256)S(1)} %rsqrt.22, pred[]{:T(512)S(6)} %eq.2, bf16[6,32,4096]{2,1,0:T(8,128)(2,1)S(1)} %copy-done), kind=kLoop, calls=%fused_computation.14 | loop fusion | flops 7864320 | bytes 7865857 | tf_op jit(solution)/shard_map/jit(_where)/select_n | solution.py:316
  156.5 3.3 %gather_fusion = bf16[6,32,4096]{2,1,0:T(8,128)(2,1)} fusion(bf16[6,32,4096]{2,1,0:T(8,128)(2,1)} %bitcast.59, s32[1024]{0:T(1024)S(1)} %pad_clamp_fusion), kind=kCustom, calls=%fused_computation | custom fusion | bytes 3145752 | tf_op jit(solution)/shard_map/gather | solution.py:335
  159.8 0.7 copy.13
  160.5 0.6 copy.14
  (36 shorter events, 0.2 us)
Async XLA Ops:
  84.8 5.2 %copy-start.2 = (bf16[6,32,4096]{2,1,0:T(8,128)(2,1)S(1)}, bf16[6,32,4096]{2,1,0:T(8,128)(2,1)}, u32[]{:S(2)}) copy-start(bf16[6,32,4096]{2,1,0:T(8,128)(2,1)} %param.8) | copy-start | bytes 4718596
  90.0 1.0 copy-start.8
  91.0 18.2 %copy-start.3 = (bf16[16,32,128]{2,1,0:T(8,128)(2,1)}, bf16[16,32,128]{2,1,0:T(8,128)(2,1)S(1)}, u32[]{:S(2)}) copy-start(bf16[16,32,128]{2,1,0:T(8,128)(2,1)S(1)} %get-tuple-element.19) | copy-start | bytes 393220
  91.2 9.5 %copy-start.6 = (bf16[192,128]{1,0:T(8,128)(2,1)}, bf16[192,128]{1,0:T(8,128)(2,1)S(1)}, u32[]{:S(2)}) copy-start(bf16[192,128]{1,0:T(8,128)(2,1)S(1)} %convolution_convert_fusion.5) | copy-start | bytes 147460
  100.7 7.1 %slice-start = ((s8[5242880]{0:T(1024)(128)(4,1)}), s8[4194304]{0:T(1024)(128)(4,1)S(1)}, s32[]{:S(2)}) async-start(s8[5242880]{0:T(1024)(128)(4,1)} %bitcast.51), calls=%async_computation | async-start | bytes 8388608
  100.7 6.3 %copy-start = (bf16[6,32,4096]{2,1,0:T(8,128)(2,1)S(1)}, bf16[6,32,4096]{2,1,0:T(8,128)(2,1)}, u32[]{:S(2)}) copy-start(bf16[6,32,4096]{2,1,0:T(8,128)(2,1)} %param.7) | copy-start | bytes 4718596
  100.7 7.1 %slice-start.1 = ((s8[5242880]{0:T(1024)(128)(4,1)}), s8[1048576]{0:T(1024)(128)(4,1)S(1)}, s32[]{:S(2)}) async-start(s8[5242880]{0:T(1024)(128)(4,1)} %bitcast.51), calls=%async_computation.1 | async-start | bytes 2097152
  109.3 6.7 %copy-start.5 = (f32[192,640]{1,0:T(8,128)}, f32[192,640]{1,0:T(8,128)S(1)}, u32[]{:S(2)}) copy-start(f32[192,640]{1,0:T(8,128)S(1)} %fusion.32) | copy-start | bytes 1474564
  116.0 4.5 %copy-start.1 = (bf16[16,256,512]{2,1,0:T(8,128)(2,1)S(1)}, bf16[16,256,512]{2,1,0:T(8,128)(2,1)}, u32[]{:S(2)}) copy-start(bf16[16,256,512]{2,1,0:T(8,128)(2,1)} %get-tuple-element.17) | copy-start | bytes 12582916
  120.4 1.0 copy-start.4
  129.9 19.6 %copy-start.7 = (bf16[192,128]{1,0:T(8,128)(2,1)S(1)}, bf16[192,128]{1,0:T(8,128)(2,1)}, u32[]{:S(2)}) copy-start(bf16[192,128]{1,0:T(8,128)(2,1)} %convolution_convert_fusion.4) | copy-start | bytes 147460
  154.0 2.5 %copy-start.11 = (s32[6]{0:T(128)S(1)}, s32[6]{0:T(128)}, u32[]{:S(2)}) copy-start(s32[6]{0:T(128)} %param.9) | copy-start | bytes 76
  156.5 3.3 %copy-start.9 = (f32[256,128]{1,0:T(8,128)S(1)}, f32[256,128]{1,0:T(8,128)}, u32[]{:S(2)}) copy-start(f32[256,128]{1,0:T(8,128)} %get-tuple-element.11) | copy-start | bytes 393220
  156.5 4.0 %copy-start.10 = (f32[32,128]{1,0:T(8,128)S(1)}, f32[32,128]{1,0:T(8,128)}, u32[]{:S(2)}) copy-start(f32[32,128]{1,0:T(8,128)} %get-tuple-element.12) | copy-start | bytes 49156

commit v4 on v3

--- a/solution.py
+++ b/solution.py
@@ -244,6 +244,168 @@
     return lax.dot_general(left, right, (dims, ((), ())), preferred_element_type=jnp.float32)
 
 
+def layers_kernel(
+    sections, width, order_ref, tok_ref, cot_ref, wa_any, wo_any, up_any, out_ref, parts_ref,
+    wa, wo, up, states, normed, low, cats, wide, flow, acc, sems,
+):
+    rows, features = tok_ref.shape
+    micro = out_ref.shape[0]
+    step = width
+    steps = features // step
+    position = lax.axis_index("section")
+    bf16, f32 = jnp.bfloat16, jnp.float32
+    pending = {}
+    for layer in range(sections):
+        for kind, (source, target) in enumerate(((wa_any, wa), (up_any, up), (wo_any, wo))):
+            copy = pltpu.make_async_copy(
+                source.at[layer], target.at[layer], sems.at[layer * 3 + kind]
+            )
+            copy.start()
+            pending[layer, kind] = copy
+
+    def ready(layer, kind):
+        if (layer, kind) in pending:
+            pending.pop((layer, kind)).wait()
+
+    def span(index):
+        return pl.ds(pl.multiple_of(index * step, step), step)
+
+    def loop(action, start):
+        return lax.fori_loop(0, steps, action, start)
+
+    zero = jnp.zeros((rows, 1), f32)
+
+    def state(layer):
+        return tok_ref if layer == 0 else states.at[layer - 1]
+
+    def squares(index, total):
+        piece = tok_ref[:, span(index)].astype(f32)
+        return total + jnp.sum(piece * piece, axis=1, keepdims=True)
+
+    total = loop(squares, zero)
+    inverses = []
+    for layer in range(sections):
+        last = layer == sections - 1
+        inverse = lax.rsqrt(total / features + epsilon)
+        inverses.append(inverse)
+        ready(layer, 0)
+        start = width if last else 0
+        acc[...] = jnp.zeros_like(acc)
+
+        def project(index, carry, layer=layer, inverse=inverse, start=start):
+            piece = (state(layer)[:, span(index)].astype(f32) * inverse).astype(bf16)
+            normed[layer, :, span(index)] = piece
+            acc[:, start:] += widen_dot(piece, wa[layer, span(index), start:])
+            return carry
+
+        loop(project, 0)
+        low[layer] = acc[:, width:].astype(bf16)
+        ready(layer, 1)
+        ready(layer, 2)
+        if not last:
+            values = (acc[:, :width] + widen_dot(low[layer], up[layer], ((1,), (1,)))).astype(bf16)
+            cats[layer, :, :width] = values
+
+            def widen(index, carry, layer=layer):
+                added = widen_dot(cats[layer, :, :width], wo[layer, span(index), :], ((1,), (1,)))
+                piece = (state(layer)[:, span(index)].astype(f32) + added).astype(bf16)
+                states[layer, :, span(index)] = piece
+                back = piece.astype(f32)
+                return carry + jnp.sum(back * back, axis=1, keepdims=True)
+
+            total = loop(widen, zero)
+
+    def backward(layer):
+        upstream = cot_ref if layer == sections - 1 else flow.at[layer + 1]
+        inverse = inverses[layer]
+        acc[:, :width] = jnp.zeros((rows, width), f32)
+
+        def narrow(index, carry):
+            acc[:, :width] += widen_dot(upstream[:, span(index)], wo[layer, span(index), :])
+            return carry
+
+        loop(narrow, 0)
+        d_values = acc[:, :width].astype(bf16)
+        cats[layer, :, :width] = d_values
+        cats[layer, :, width:] = widen_dot(d_values, up[layer]).astype(bf16)
+
+        def open_up(index, carry):
+            piece = widen_dot(cats[layer], wa[layer, span(index), :], ((1,), (1,)))
+            wide[:, span(index)] = piece
+            inputs = state(layer)[:, span(index)].astype(f32)
+            return carry + jnp.sum(piece * inputs, axis=1, keepdims=True)
+
+        mean = loop(open_up, zero) / features
+
+        def finish(index, carry):
+            inputs = state(layer)[:, span(index)].astype(f32)
+            piece = upstream[:, span(index)].astype(f32) + inverse * (
+                wide[:, span(index)] - inputs * inverse * inverse * mean
+            )
+            flow[layer, :, span(index)] = piece.astype(bf16)
+            return carry
+
+        loop(finish, 0)
+
+    for layer in reversed(range(sections)):
+        if layer == sections - 1:
+            backward(layer)
+        else:
+            pl.when(position <= layer)(functools.partial(backward, layer))
+
+    blocks = parts_ref.shape[0]
+    share, share_up = features // blocks, width // blocks
+
+    def contract(index, carry):
+        columns = pl.ds(pl.multiple_of(index * share, share), share)
+        parts_ref[index, :share, :] = widen_dot(
+            normed[position, :, columns], cats[position, :, width:], ((0,), (0,))
+        ).astype(bf16)
+        return carry
+
+    lax.fori_loop(0, blocks, contract, 0)
+    both = widen_dot(cats[position, :, :width], low[position], ((0,), (0,))).astype(bf16)
+    for index in range(blocks):
+        parts_ref[index, share:, :] = both[index * share_up:(index + 1) * share_up]
+    local = rows // micro
+    for slot in range(micro):
+        out_ref[slot] = flow[position, pl.ds(pl.multiple_of(order_ref[slot] * local, local), local), :]
+
+
+def run_layers(tokens, cotangent, order, joined, proj, up):
+    micro, local, features = tokens.shape
+    sections, _, width = proj.shape
+    rank = up.shape[2]
+    rows = micro * local
+    shares = lax.axis_size("fsdp")
+    block = (features + width) // shares
+    bf16, f32 = jnp.bfloat16, jnp.float32
+    inside, outside = pl.BlockSpec(memory_space=pltpu.VMEM), pl.BlockSpec(memory_space=pl.ANY)
+    return pl.pallas_call(
+        functools.partial(layers_kernel, sections, width),
+        out_shape=[
+            jax.ShapeDtypeStruct((micro, local, features), bf16),
+            jax.ShapeDtypeStruct((shares, block, rank), bf16),
+        ],
+        in_specs=[pl.BlockSpec(memory_space=pltpu.SMEM), inside, inside] + [outside] * 3,
+        out_specs=[inside, inside],
+        scratch_shapes=[
+            pltpu.VMEM(joined.shape, bf16),
+            pltpu.VMEM(proj.shape, bf16),
+            pltpu.VMEM(up.shape, bf16),
+            pltpu.VMEM((sections - 1, rows, features), bf16),
+            pltpu.VMEM((sections, rows, features), bf16),
+            pltpu.VMEM((sections, rows, rank), bf16),
+            pltpu.VMEM((sections, rows, width + rank), bf16),
+            pltpu.VMEM((rows, features), f32),
+            pltpu.VMEM((sections, rows, features), bf16),
+            pltpu.VMEM((rows, width + rank), f32),
+            pltpu.SemaphoreType.DMA((sections * 3,)),
+        ],
+        compiler_params=pltpu.CompilerParams(vmem_limit_bytes=56 * 2**20),
+    )(order, tokens.reshape(rows, features), cotangent.reshape(rows, features), joined, proj, up)
+
+
 def custom_route():
     fsdp = lax.axis_size("fsdp")
     return lax.axis_size("section") == 2 and fsdp % 4 == 0 and fsdp <= 16
@@ -273,6 +435,14 @@
     micro, local, features = tokens.shape
     width = w_value.shape[2]
     joined, proj, up = gather_weights(w_value, w_out, adapter_down, adapter_up)
+
+    if custom_route():
+        out, parts = run_layers(tokens, cotangent, order, joined, proj, up)
+        shares = lax.axis_size("fsdp")
+        grad_down, grad_up = settle(
+            parts.reshape(shares // 2, 2, *parts.shape[1:]), features // shares
+        )
+        return (out[None], grad_down[None], grad_up.T[None])
 
     current = tokens.reshape(micro * local, features)
     saved = []
@@ -326,12 +496,8 @@
         [part_down.reshape(shares, -1, rank), part_up.reshape(shares, -1, rank)], axis=1
     )
     share_down = features // shares
-    if custom_route():
-        split = parts.astype(jnp.bfloat16).reshape(shares // 2, 2, *parts.shape[1:])
-        grad_down, grad_up = settle(split, share_down)
-    else:
-        combined = lax.psum_scatter(parts, "fsdp", scatter_dimension=0, tiled=True)[0]
-        grad_down, grad_up = combined[:share_down], combined[share_down:]
+    combined = lax.psum_scatter(parts, "fsdp", scatter_dimension=0, tiled=True)[0]
+    grad_down, grad_up = combined[:share_down], combined[share_down:]
     out = mine(grads).reshape(micro, local, features)[order]
     return (out[None], grad_down[None], grad_up.T[None])
 

time: 162 us -> 138 us (0.85)
  Pallas kernels: 97.8 us -> 130 us
  matrix products: 29.4 us -> 0 us
  local copies, waits for them, and re-layouts: 21.2 us -> 4.7 us
  other arithmetic: 11.8 us -> 1.74 us
    pallas_call x0 -> x1, Pallas kernels: none -> 32.2 us  [run_layers(): pl.pallas_call(functools.partial(layers_kernel, sections, width), out_sha...]
    dot_general x10 -> x0, matrix products: 29.4 us -> none  [widen_dot(): lax.dot_general(left, right, (dims, ((), ())), preferred_element_type=jnp...]
    slice x3 -> x0, local copies, waits for them, and re-layouts: 14.7 us -> none  [the longest x1 9.47 us: body(): both = widen_dot(normed, joined[layer])]
    convert_element_type x2 -> x0, other arithmetic: 4.8 us -> none  [the longest x1 4.42 us: body(): upstream = (upstream.astype(jnp.float32) + inverse * (d_normed - widened...]
    gather x1 -> x0, local copies, waits for them, and re-layouts: 3.29 us -> none  [body(): out = mine(grads).reshape(micro, local, features)[order]]
    select_n x2 -> x0, other arithmetic: 2.47 us -> none  [the longest x1 2.46 us: mine(): chosen = jnp.where(position == layer, items[layer], chosen)]
    concatenate x1 -> x0, other arithmetic: 2.42 us -> none  [body(): jnp.concatenate([part_down.reshape(shares, -1, rank), part_up.reshape(sha...]
    unnamed x31 -> x3, local copies, waits for them, and re-layouts: 3.17 us -> 4.7 us
where the time goes in v4:
time: 138 us; the launch traced here: 137 us
  Pallas kernels  130 us (94%)
  local copies, waits for them, and re-layouts  4.7 us (3%)
  other arithmetic  1.74 us (1%)
    pallas_call x1, Pallas kernels, spread(): pl.pallas_call(functools.partial(spread_kernel, fsdp // 4, plan), out_sha...  80.6 us
    pallas_call x1, Pallas kernels, run_layers(): pl.pallas_call(functools.partial(layers_kernel, sections, width), out_sha...  32.2 us
    pallas_call x1, Pallas kernels, settle(): pl.pallas_call(settle_kernel, out_shape=[jax.ShapeDtypeStruct((split, ran...  17.2 us
    unnamed x3, local copies, waits for them, and re-layouts  4.7 us

profile of v4, /device:TPU:0, one launch (start us, length us, event | category | flops | bytes accessed | tf_op | source)
XLA Modules:
  0.0 137.1 jit_solution(14443482927655761916)
XLA Ops:
  0.6 1.8 %copy.10 = bf16[1,512,256]{1,2,0:T(8,128)(2,1)} copy(bf16[1,512,256]{2,1,0:T(8,128)(2,1)} %param.11) | data formatting | bytes 524288 | tf_op args[4]
  2.4 1.7 %pad_maximum_fusion.a_ref = bf16[256,640]{1,0:T(8,128)(2,1)} fusion(bf16[256,128]{1,0:T(8,128)(2,1)} %bitcast.28, bf16[256,512]{1,0:T(8,128)(2,1)} %bitcast.26), kind=kLoop, calls=%fused_computation | loop fusion | flops 655360 | bytes 655360 | tf_op jit(solution)/shard_map/concatenate | solution.py:416
  4.2 80.6 %shard_map.94 = (bf16[32,256,640]{2,1,0:T(8,128)(2,1)}, bf16[32,256,512]{2,1,0:T(8,128)(2,1)}, bf16[32,32,128]{2,1,0:T(8,128)(2,1)}) custom-call(bf16[256,640]{1,0:T(8,128)(2,1)} %pad_maximum_fusion.a_ref, bf16[256,512]{1,0:T(8,128)(2,1)} %bitcast.24, bf16[32,128]{1,0:T(8,128)(2,1)} %bitcast.30), custom_call_target="tpu_custom_call" | custom-call | tf_op jit(solution)/shard_map/pallas_call | solution.py:159
  84.8 32.2 %shard_map.95 = (bf16[6,32,4096]{2,1,0:T(8,128)(2,1)}, bf16[16,288,128]{2,1,0:T(8,128)(2,1)}) custom-call(s32[6]{0:T(128)} %order_ref.1, bf16[192,4096]{1,0:T(8,128)(2,1)} %bitcast.21, bf16[192,4096]{1,0:T(8,128)(2,1)} %bitcast.22, bf16[2,4096,640]{2,1,0:T(8,128)(2,1)} %bitcast.19, bf16[2,4096,512]{2,1,0:T(8,128)(2,1)} %bitcast.20, bf16[2,512,128]{2,1,0:T(8,128)(2,1)} %bitcast.25), custom_call_target="tpu_custom_call" | custom-call | tf_op jit(solution)/shard_map/pallas_call | solution.py:384
  117.0 17.2 %shard_map.96 = (f32[256,128]{1,0:T(8,128)}, f32[32,128]{1,0:T(8,128)}) custom-call(bf16[8,2,288,128]{3,2,1,0:T(8,128)(2,1)} %bitcast.23), custom_call_target="tpu_custom_call" | custom-call | tf_op jit(solution)/shard_map/pallas_call | solution.py:230
  134.2 1.6 %copy.13 = f32[1,256,128]{2,1,0:T(8,128)} copy(f32[1,256,128]{2,1,0:T(8,128)} %bitcast.27) | data formatting | bytes 262144
  135.7 1.3 copy.14
